TPU v7x, 256 devices: a whole 4x4x8 slice. The times are simulated.
256 devices in a mesh: seq: 64 (over y, x_lo, z), dp: 4 (over x_hi, core).
Axes of the slice: x: 4 (x_hi: 2, x_lo: 2; x = x_hi * 2 + x_lo), y: 4, z: 8, core: 2. Of those that a mesh axis runs over, the one named last changes fastest.
Arguments:
- queries: bfloat16 [4, 16384, 2048], P('dp', 'seq'), may hold values from -12 to 12
- keys: bfloat16 [4, 16384, 1024], P('dp', 'seq'), may hold values from -6 to 6
- values: bfloat16 [4, 16384, 1024], P('dp', 'seq'), may hold values from -6 to 6
- out_grad: bfloat16 [4, 16384, 1792], P('dp', 'seq'), may hold values from -6 to 6
- out_weight: bfloat16 [2048, 1792], P('seq'), may hold values from -0.125 to 0.125
- seq_len: int32 [4], P('dp'), may hold values from 4096 to 16384, as said below
Outputs:
- query_grad: bfloat16 [4, 16384, 2048], P('dp', 'seq')
- key_grad: bfloat16 [4, 16384, 1024], P('dp', 'seq')
- value_grad: bfloat16 [4, 16384, 1024], P('dp', 'seq')
- weight_grad: float32 [2048, 1792], P('seq')
- grad_rms: float32 [], replicated
Inputs may be any that keep to these rules, and one draw needn't show every extreme that they name: `seq_len`: at least one sequence has the full length 16384.
All inputs are finite; a program needn't handle non-finite values.
Results may differ from a plain program's by a relative error of at most 0.014.
Values may be sent and summed in bfloat16 or wider, within the bound.
A program may use at most 128 MiB of HBM per device.

v0:
```python
import functools

import jax
import jax.numpy as jnp
from jax import lax
from jax.sharding import Mesh
from jax.sharding import PartitionSpec as P

HEADS = 8
KV_HEADS = 4
HEAD_DIM = 256
D_OUT = 1792
WINDOW = 512
TOK_DEV = 256
SEQ = ("seq_0", "seq_1", "seq_2")
DP = ("dp_0", "dp_1")
SEQ_DP = ("seq_0", "seq_1", "seq_2", "dp_0", "dp_1")


SCALE = 0.0625
CAP = 50.0


def shifted(value, axis, steps):
    count = lax.axis_size(axis)
    initial, last = (max(0, -steps), min(count, count - steps))
    return lax.ppermute(value, axis, [(source, source + steps) for source in range(initial, last)])


def copy_for_each(value, axis):
    size = lax.axis_size(axis)
    return lax.all_to_all(
        jnp.broadcast_to(value[None], (size, *value.shape)), axis, 0, 0, tiled=True
    )


def taken_together(value, axis):
    everything = copy_for_each(value, axis)
    return jnp.sum(everything.astype(jnp.float32), axis=0)


def over_axes(value, axes):
    return functools.reduce(lax.psum, axes, value)


def band_block(q_rows, k_rows, v_rows, g_rows, q_pos, k_pos):
    count = q_rows.shape[0]
    span = k_rows.shape[0]
    group = HEADS // KV_HEADS
    qh = q_rows.reshape(count, KV_HEADS, group, HEAD_DIM)
    kh = k_rows.reshape(span, KV_HEADS, HEAD_DIM)
    vh = v_rows.reshape(span, KV_HEADS, HEAD_DIM)
    gh = g_rows.reshape(count, KV_HEADS, group, HEAD_DIM)
    raw = jnp.einsum("tkgd,jkd->kgtj", qh, kh, preferred_element_type=jnp.float32) * SCALE
    capped = CAP * jnp.tanh(raw / CAP)
    allowed = (
        (k_pos[None, :] >= 0)
        & (k_pos[None, :] <= q_pos[:, None])
        & (k_pos[None, :] > q_pos[:, None] - WINDOW)
    )
    expo = jnp.where(allowed, jnp.exp(capped), jnp.zeros((), jnp.float32))
    probs = expo / jnp.sum(expo, axis=-1, keepdims=True)
    probs_b = probs.astype(jnp.bfloat16)
    attn = jnp.einsum("kgtj,jkd->tkgd", probs_b, vh, preferred_element_type=jnp.float32).astype(
        jnp.bfloat16
    )
    delta = jnp.einsum("tkgd,tkgd->kgt", gh, attn, preferred_element_type=jnp.float32)[..., None]
    dprob = jnp.einsum("tkgd,jkd->kgtj", gh, vh, preferred_element_type=jnp.float32)
    dscore = (probs * (dprob - delta) * (1.0 - (capped / CAP) ** 2) * SCALE).astype(jnp.bfloat16)
    dq = jnp.einsum("kgtj,jkd->tkgd", dscore, kh, preferred_element_type=jnp.float32).reshape(
        count, -1
    )
    dk = jnp.einsum("kgtj,tkgd->jkd", dscore, qh, preferred_element_type=jnp.float32).reshape(
        span, -1
    )
    dv = jnp.einsum("kgtj,tkgd->jkd", probs_b, gh, preferred_element_type=jnp.float32).reshape(
        span, -1
    )
    return (dq, dk, dv, attn.reshape(count, -1))


def shards(queries, keys, values, out_grad, out_weight, seq_len):
    q_rows = queries[0]
    k_rows = keys[0]
    v_rows = values[0]
    length = seq_len[0]
    seq_devices = lax.axis_size(SEQ)
    rep_devices = lax.axis_size(DP)
    start = lax.axis_index(SEQ) * TOK_DEV
    positions = start + jnp.arange(TOK_DEV, dtype=jnp.int32)
    valid = positions < length
    masked = jnp.where(valid[:, None], out_grad[0], jnp.zeros((), jnp.bfloat16))
    grad_attn = lax.dot_general(
        masked,
        lax.all_gather(out_weight, SEQ, axis=0, tiled=True),
        (((1,), (1,)), ((), ())),
        preferred_element_type=jnp.float32,
    ).astype(jnp.bfloat16)
    reach = (WINDOW + TOK_DEV - 2) // TOK_DEV
    lead = reach * TOK_DEV
    key_parts = []
    val_parts = []
    for back in range(reach, 0, -1):
        earlier_k, earlier_v = shifted((k_rows, v_rows), SEQ, back)
        key_parts.append(earlier_k)
        val_parts.append(earlier_v)
    key_block = jnp.concatenate(key_parts + [k_rows], 0)
    val_block = jnp.concatenate(val_parts + [v_rows], 0)
    k_pos = start - lead + jnp.arange(lead + TOK_DEV, dtype=jnp.int32)
    dq_raw, dk_all, dv_all, attn = band_block(
        q_rows, key_block, val_block, grad_attn, positions, k_pos
    )
    dk_raw = dk_all[lead:]
    dv_raw = dv_all[lead:]
    for back in range(1, reach + 1):
        first = (reach - back) * TOK_DEV
        later_k, later_v = (
            shifted(dk_all[first : first + TOK_DEV].astype(jnp.bfloat16), SEQ, -back).astype(
                jnp.float32
            ),
            shifted(dv_all[first : first + TOK_DEV].astype(jnp.bfloat16), SEQ, -back).astype(
                jnp.float32
            ),
        )
        dk_raw = dk_raw + later_k
        dv_raw = dv_raw + later_v
    width = HEADS * HEAD_DIM
    part = lax.psum_scatter(
        lax.dot_general(attn, masked, (((0,), (0,)), ((), ())), preferred_element_type=jnp.float32),
        SEQ,
        scatter_dimension=0,
        tiled=True,
    )
    weight_raw = taken_together(part.astype(jnp.bfloat16), DP).astype(jnp.float32)
    weight_sq = jnp.sum(weight_raw * weight_raw) / rep_devices
    own_count = jnp.clip(length - start, 0, TOK_DEV)
    slots = TOK_DEV * seq_devices * rep_devices
    entries = slots * (HEADS + 2 * KV_HEADS) * HEAD_DIM + width * D_OUT
    act_sq = jnp.sum(dq_raw * dq_raw) + jnp.sum(dk_raw * dk_raw) + jnp.sum(dv_raw * dv_raw)
    total, act_total, weight_total = (
        over_axes(own_count.astype(jnp.float32), SEQ_DP),
        over_axes(act_sq, SEQ_DP),
        over_axes(weight_sq, SEQ_DP),
    )
    act_scale = slots / total
    weight_scale = lax.rsqrt(total)
    dq_s = dq_raw * act_scale
    dk_s = dk_raw * act_scale
    dv_s = dv_raw * act_scale
    squares = act_total * (act_scale * act_scale) + weight_total * (weight_scale * weight_scale)
    grad_rms = jnp.sqrt(squares / entries)
    weight_grad = weight_raw * weight_scale
    return (
        dq_s.astype(jnp.bfloat16)[None],
        dk_s.astype(jnp.bfloat16)[None],
        dv_s.astype(jnp.bfloat16)[None],
        weight_grad,
        grad_rms,
    )


def solution(mesh):
    split = Mesh(mesh.devices.reshape(4, 2, 8, 2, 2), ("seq_0", "seq_1", "seq_2", "dp_0", "dp_1"))
    placed = (
        P(DP, SEQ, None),
        P(DP, SEQ, None),
        P(DP, SEQ, None),
        P(DP, SEQ, None),
        P(SEQ, None),
        P(DP),
    )
    return jax.shard_map(
        shards,
        mesh=split,
        in_specs=placed,
        out_specs=(P(DP, SEQ, None), P(DP, SEQ, None), P(DP, SEQ, None), P(SEQ, None), P()),
        check_vma=False,
    )
```

profile of v0, /device:TPU:1, one launch (start us, length us, event | category | flops | bytes accessed | tf_op | source)
XLA Modules:
  0.0 783.0 jit_solution(6166765927309741051)
XLA Ops:
  9.2 5.2 collective-permute-start.3
  14.4 4.9 collective-permute-start.2
  20.5 5.6 collective-permute-start.1
  26.1 2.3 collective-permute-start
  32.0 2.2 copy.64
  34.2 8.4 %collective-permute-done.2 = bf16[256,1024]{0,1:T(8,128)(2,1)} collective-permute-done((bf16[256,1024]{0,1:T(8,128)(2,1)S(1)}, bf16[256,1024]{0,1:T(8,128)(2,1)}, u32[]{:S(2)}, u32[]{:S(2)}) %collective-permute-start.2) | collective-permute-done | bytes 524320 | tf_op jit(solution)/shard_map/ppermute | solution.py:27
  42.6 2.1 copy.63
  44.6 22.7 %collective-permute-done.1 = bf16[256,1024]{0,1:T(8,128)(2,1)} collective-permute-done((bf16[256,1024]{0,1:T(8,128)(2,1)S(1)}, bf16[256,1024]{0,1:T(8,128)(2,1)}, u32[]{:S(2)}, u32[]{:S(2)}) %collective-permute-start.1) | collective-permute-done | bytes 524320 | tf_op jit(solution)/shard_map/ppermute | solution.py:27
  67.4 1.3 copy.58
  68.6 17.5 %collective-permute-done = bf16[256,1024]{0,1:T(8,128)(2,1)} collective-permute-done((bf16[256,1024]{0,1:T(8,128)(2,1)S(1)}, bf16[256,1024]{0,1:T(8,128)(2,1)}, u32[]{:S(2)}, u32[]{:S(2)}) %collective-permute-start) | collective-permute-done | bytes 524320 | tf_op jit(solution)/shard_map/ppermute | solution.py:27
  86.2 1.2 copy.57
  87.4 2.0 fusion.4
  89.4 2.6 copy-done
  92.0 1.8 fusion.5
  93.8 195.2 %all-gather.2.cloned.1.call-done = bf16[2048,1792]{1,0:T(8,128)(2,1)} async-done(((bf16[32,1792]{1,0:T(8,128)(2,1)}), bf16[2048,1792]{1,0:T(8,128)(2,1)}) %all-gather.2.cloned.1.call-update) | async-done | bytes 7340048 | tf_op jit(solution)/shard_map/all_gather | solution.py:95
  289.0 6.5 convolution_convert_fusion
  295.5 2.6 reshape.85
  298.1 3.3 bitcast_convert_fusion
  301.4 4.1 copy.91
  305.6 3.2 multiply_reduce_fusion
  308.8 7.4 fusion.6
  316.2 3.6 copy.76
  319.8 6.8 fusion.1
  326.7 2.6 fusion.27
  330.4 2.0 copy.73
  332.4 2.0 copy.75
  334.5 1.3 collective-permute-start.5
  335.8 1.3 collective-permute-start.4
  337.1 3.9 fusion.28
  343.1 1.3 collective-permute-start.7
  344.4 1.3 collective-permute-start.6
  345.7 1.3 slice.40
  347.3 1.3 slice.43
  349.0 5.4 multiply_reduce_fusion.1
  354.3 302.3 %reduce-scatter.2.cloned.1.call-done = f32[32,1792]{1,0:T(8,128)} async-done(((f32[2048,1792]{1,0:T(8,128)}), f32[32,1792]{1,0:T(8,128)}) %reduce-scatter.2.cloned.1.call-update) | async-done | bytes 229392 | tf_op jit(solution)/shard_map/reduce_scatter | solution.py:128
  658.4 55.7 %all-to-all-start = ((bf16[4,32,1792]{2,1,0:T(8,128)(2,1)}), bf16[4,32,1792]{2,1,0:T(8,128)(2,1)S(1)}, u32[]{:S(2)}, u32[]{:S(2)}) async-start(bf16[4,32,1792]{2,1,0:T(8,128)(2,1)} %broadcast_in_dim.53), calls=%async_computation.1 | async-start | bytes 917504 | tf_op jit(solution)/shard_map/all_to_all | solution.py:32
  714.2 2.1 multiply_reduce_fusion.3
  717.6 2.1 multiply_reduce_fusion.2
  720.3 2.5 all-to-all-done
  724.2 6.5 all-reduce.1
  730.7 4.4 all-reduce.4
  735.1 11.4 %all-reduce = (f32[]{:T(128)}, f32[]{:T(128)}, f32[]{:T(128)}) all-reduce(f32[]{:T(128)} %get-tuple-element.32, f32[]{:T(128)} %get-tuple-element.33, f32[]{:T(128)} %get-tuple-element.34), channel_id=1, replica_groups=mesh['seq_0'=4,'seq_1'=2,'seq_2'=8,'dp_0'=2,'dp_1'=2] {'seq_2'}, use_global_device_ids=true, to_apply=%region_3.4 | all-reduce | flops 3 | bytes 24 | tf_op jit(solution)/shard_map/psum | solution.py:43
  746.5 5.9 all-reduce.3
  752.4 11.5 %all-reduce.2 = (f32[]{:T(128)}, f32[]{:T(128)}, f32[]{:T(128)}) all-reduce(f32[]{:T(128)} %get-tuple-element.29, f32[]{:T(128)} %get-tuple-element.30, f32[]{:T(128)} %get-tuple-element.31), channel_id=1, replica_groups=mesh['seq_0'=4,'seq_1'=2,'seq_2'=8,'dp_0'=2,'dp_1'=2] {'dp_1'}, use_global_device_ids=true, to_apply=%region_5.6 | all-reduce | flops 3 | bytes 24 | tf_op jit(solution)/shard_map/psum | solution.py:43
  767.4 1.8 multiply_convert_fusion
  769.2 1.4 copy.81
  770.6 2.2 fusion.14
  772.8 2.2 fusion.13
  (47 shorter events, 13.2 us)
Async XLA Ops:
  7.2 23.9 %copy-start.4 = (bf16[1,256,2048]{2,1,0:T(8,128)(2,1)S(1)}, bf16[1,256,2048]{2,1,0:T(8,128)(2,1)}, u32[]{:S(2)}) copy-start(bf16[1,256,2048]{2,1,0:T(8,128)(2,1)} %param.6) | copy-start | bytes 3145732
  7.2 281.8 %all-gather.2.cloned.1.call-start = ((), (), s32[]{:S(2)}) async-start(), calls=%async_computation.2 | async-start | bytes 7454720 | tf_op jit(solution)/shard_map/all_gather | solution.py:95
  7.9 648.8 %reduce-scatter.2.cloned.1.call-start = ((), (), s32[]{:S(2)}) async-start(), calls=%async_computation.3 | async-start | bytes 14909440 | tf_op jit(solution)/shard_map/reduce_scatter | solution.py:128
  9.2 22.8 %collective-permute-start.3 = (bf16[256,1024]{0,1:T(8,128)(2,1)S(1)}, bf16[256,1024]{0,1:T(8,128)(2,1)}, u32[]{:S(2)}, u32[]{:S(2)}) collective-permute-start(bf16[256,1024]{0,1:T(8,128)(2,1)S(1)} %bitcast.113), channel_id=1, source_target_pairs={{0,4},{4,8},{8,12},{12,16},{16,20},{20,24},{24,28},{28,32},{32,36}... | collective-permute-start | bytes 1572872 | tf_op jit(solution)/shard_map/ppermute | solution.py:27
  14.4 28.2 %collective-permute-start.2 = (bf16[256,1024]{0,1:T(8,128)(2,1)S(1)}, bf16[256,1024]{0,1:T(8,128)(2,1)}, u32[]{:S(2)}, u32[]{:S(2)}) collective-permute-start(bf16[256,1024]{0,1:T(8,128)(2,1)S(1)} %bitcast.114), channel_id=1, source_target_pairs={{0,8},{4,12},{8,16},{12,20},{16,24},{20,28},{24,32},{28,36},{32,40... | collective-permute-start | bytes 1572872 | tf_op jit(solution)/shard_map/ppermute | solution.py:27
  20.5 46.9 %collective-permute-start.1 = (bf16[256,1024]{0,1:T(8,128)(2,1)S(1)}, bf16[256,1024]{0,1:T(8,128)(2,1)}, u32[]{:S(2)}, u32[]{:S(2)}) collective-permute-start(bf16[256,1024]{0,1:T(8,128)(2,1)S(1)} %bitcast.110), channel_id=1, source_target_pairs={{0,4},{4,8},{8,12},{12,16},{16,20},{20,24},{24,28},{28,32},{32,36}... | collective-permute-start | bytes 1572872 | tf_op jit(solution)/shard_map/ppermute | solution.py:27
  26.1 60.1 %collective-permute-start = (bf16[256,1024]{0,1:T(8,128)(2,1)S(1)}, bf16[256,1024]{0,1:T(8,128)(2,1)}, u32[]{:S(2)}, u32[]{:S(2)}) collective-permute-start(bf16[256,1024]{0,1:T(8,128)(2,1)S(1)} %bitcast.111), channel_id=1, source_target_pairs={{0,8},{4,12},{8,16},{12,20},{16,24},{20,28},{24,32},{28,36},{32,40... | collective-permute-start | bytes 1572872 | tf_op jit(solution)/shard_map/ppermute | solution.py:27
  31.6 57.8 %copy-start.1 = (bf16[1,256,2048]{1,2,0:T(8,128)(2,1)}, bf16[1,256,2048]{1,2,0:T(8,128)(2,1)S(1)}, u32[]{:S(2)}) copy-start(bf16[1,256,2048]{1,2,0:T(8,128)(2,1)S(1)} %copy.102) | copy-start | bytes 3145732
  31.6 55.8 %copy-start.6 = (bf16[256,4,256]{2,0,1:T(8,128)(2,1)S(1)}, bf16[256,4,256]{2,0,1:T(8,128)(2,1)}, u32[]{:S(2)}) copy-start(bf16[256,4,256]{2,0,1:T(8,128)(2,1)} %copy.59) | copy-start | bytes 1572868
  68.6 20.8 %copy-start.7 = (bf16[256,4,256]{2,0,1:T(8,128)(2,1)}, bf16[256,4,256]{2,0,1:T(8,128)(2,1)S(1)}, u32[]{:S(2)}) copy-start(bf16[256,4,256]{2,0,1:T(8,128)(2,1)S(1)} %copy.58) | copy-start | bytes 1572868
  87.4 2.0 copy-start.8
  89.4 2.6 copy-start
  305.6 3.2 copy-start.5
  319.8 6.9 copy-start.2
  326.7 2.6 copy-start.3
  334.5 379.7 %collective-permute-start.5 = (bf16[256,1024]{1,0:T(8,128)(2,1)}, bf16[256,1024]{1,0:T(8,128)(2,1)}, u32[]{:S(2)}, u32[]{:S(2)}) collective-permute-start(bf16[256,1024]{1,0:T(8,128)(2,1)} %copy.75), channel_id=1, source_target_pairs={{8,0},{12,4},{16,8},{20,12},{24,16},{28,20},{32,24},{36,28},{40,32... | collective-permute-start | bytes 1572872 | tf_op jit(solution)/shard_map/ppermute | solution.py:27
  335.8 378.4 %collective-permute-start.4 = (bf16[256,1024]{1,0:T(8,128)(2,1)}, bf16[256,1024]{1,0:T(8,128)(2,1)}, u32[]{:S(2)}, u32[]{:S(2)}) collective-permute-start(bf16[256,1024]{1,0:T(8,128)(2,1)} %copy.73), channel_id=1, source_target_pairs={{4,0},{8,4},{12,8},{16,12},{20,16},{24,20},{28,24},{32,28},{36,32}... | collective-permute-start | bytes 1572872 | tf_op jit(solution)/shard_map/ppermute | solution.py:27
  343.1 374.5 %collective-permute-start.7 = (bf16[256,1024]{1,0:T(8,128)(2,1)}, bf16[256,1024]{1,0:T(8,128)(2,1)}, u32[]{:S(2)}, u32[]{:S(2)}) collective-permute-start(bf16[256,1024]{1,0:T(8,128)(2,1)} %copy.80), channel_id=1, source_target_pairs={{8,0},{12,4},{16,8},{20,12},{24,16},{28,20},{32,24},{36,28},{40,32... | collective-permute-start | bytes 1572872 | tf_op jit(solution)/shard_map/ppermute | solution.py:27
  344.4 373.2 %collective-permute-start.6 = (bf16[256,1024]{1,0:T(8,128)(2,1)}, bf16[256,1024]{1,0:T(8,128)(2,1)}, u32[]{:S(2)}, u32[]{:S(2)}) collective-permute-start(bf16[256,1024]{1,0:T(8,128)(2,1)} %copy.78), channel_id=1, source_target_pairs={{4,0},{8,4},{12,8},{16,12},{20,16},{24,20},{28,24},{32,28},{36,32}... | collective-permute-start | bytes 1572872 | tf_op jit(solution)/shard_map/ppermute | solution.py:27
  658.4 64.4 %all-to-all-start = ((bf16[4,32,1792]{2,1,0:T(8,128)(2,1)}), bf16[4,32,1792]{2,1,0:T(8,128)(2,1)S(1)}, u32[]{:S(2)}, u32[]{:S(2)}) async-start(bf16[4,32,1792]{2,1,0:T(8,128)(2,1)} %broadcast_in_dim.53), calls=%async_computation.1 | async-start | bytes 917504 | tf_op jit(solution)/shard_map/all_to_all | solution.py:32
Sparse Core Ops, SparseCore 0:
  9.8 279.1 all-gather.1
  316.3 340.3 reduce-scatter.1
where the time goes:
time: 784 us; the launch traced here: 783 us
  waiting for transfers between devices  549 us (70%)
  starting transfers between devices  78.9 us (10%)
  blocking collectives  39.8 us (5%)
  matrix products  37.8 us (5%)
  local copies, waits for them, and re-layouts  37.5 us (5%)
  between operations  21.5 us (3%)
  other arithmetic  18.2 us (2%)
    reduce_scatter x1, waiting for transfers between devices, shards(): lax.psum_scatter(lax.dot_general(attn, masked, (((0,), (0,)), ((), ())),...  302 us
    all_gather x1, waiting for transfers between devices, shards(): lax.all_gather(out_weight, SEQ, axis=0, tiled=True)  195 us
    all_to_all x1, starting transfers between devices, copy_for_each(): lax.all_to_all(jnp.broadcast_to(value[None], (size, *value.shape)), axis,...  55.7 us
    ppermute x8, waiting for transfers between devices, shifted(): lax.ppermute(value, axis, [(source, source + steps) for source in range(i...  48.6 us
    psum x5, blocking collectives, over_axes(): return functools.reduce(lax.psum, axes, value)  39.8 us
    ppermute x8, starting transfers between devices, shifted(): lax.ppermute(value, axis, [(source, source + steps) for source in range(i...  23.1 us
  transfers between devices with their start and end apart: 11, of which 6 were waited for; matrix products, arithmetic and copies ran while one was open for 7% of the time, Pallas kernels for 0%

commit v1 on v0

v1 whole, which is shorter than its diff:
```python
import functools

import jax
import jax.numpy as jnp
from jax import lax
from jax.experimental import pallas as pl
from jax.experimental.pallas import tpu as pltpu
from jax.sharding import Mesh
from jax.sharding import PartitionSpec as P

HEADS = 8
KV_HEADS = 4
GROUP = HEADS // KV_HEADS
HD = 256
D_OUT = 1792
WINDOW = 512
TOK = 256
SEQ = ("sy", "sx", "sz")
DP = ("dx", "dc")
AXES = ("sy", "sx", "sz", "dx", "dc")
N_DEV_SEQ = 64
SLOTS = 4 * 16384

SCALE = 0.0625
CAP = 50.0
LOG2E = 1.4426950408889634
CHANNELS = 128

F32 = jnp.float32
BF16 = jnp.bfloat16
MESH = pl.DeviceIdType.MESH


def dot_nt(a, b):
    return lax.dot_general(a, b, (((1,), (1,)), ((), ())), preferred_element_type=F32)


def dot_nn(a, b):
    return lax.dot_general(a, b, (((1,), (0,)), ((), ())), preferred_element_type=F32)


def dot_tn(a, b):
    return lax.dot_general(a, b, (((0,), (0,)), ((), ())), preferred_element_type=F32)


def col(n):
    return pl.ds(n * HD, HD)


def body(
    len_ref, q_ref, k_ref, v_ref, og_ref, w_ref, lt_ref,
    dq_ref, dk_ref, dv_ref, dw_ref, sq_ref,
    wf, k1, k2, v1, v2, mk, at, pb, pw, tw, dwm, sdb, rdb, xsb, xrb, ysb, yrb, zsb, zrb,
    fsb, frb, hsb, hrb, c2s, c2r, cms, cmr, c1, c0, lts, ssem, rsem,
):
    y, xl, z, xh, c = (lax.axis_index(a) for a in AXES)
    oc = 1 - c
    pos = (y * 2 + xl) * 8 + z

    def at_seq(s):
        return (lax.div(s, 16), lax.rem(lax.div(s, 8), 2), lax.rem(s, 8), xh, c)

    def mod(a, n):
        return lax.rem(a, n)

    right = at_seq(mod(pos + 1, N_DEV_SEQ))
    left = at_seq(mod(pos + N_DEV_SEQ - 1, N_DEV_SEQ))
    yn = (mod(y + 1, 4), xl, z, xh, c)
    yp = (mod(y + 3, 4), xl, z, xh, c)
    xr = (y, 1 - xl, z, mod(xh + xl, 2), c)
    xp = (y, 1 - xl, z, mod(xh + 1 - xl, 2), c)
    x2 = (y, xl, z, 1 - xh, c)
    x2o = (y, xl, z, 1 - xh, oc)
    cp = (y, xl, z, xh, oc)

    def zpeer(k):
        return (y, xl, mod(z + k, 8), xh, c)

    ids = {}
    sent = []

    def channel(name):
        return ids.setdefault(name, len(ids))

    def send(name, src, dst, dev):
        n = channel(name)
        d = pltpu.make_async_remote_copy(
            src_ref=src, dst_ref=dst, send_sem=ssem.at[n], recv_sem=rsem.at[n],
            device_id=dev, device_id_type=MESH,
        )
        d.start()
        sent.append(d)

    def recv(name, dst):
        n = channel(name)
        pltpu.make_async_remote_copy(
            src_ref=dst, dst_ref=dst, send_sem=ssem.at[n], recv_sem=rsem.at[n],
            device_id=cp, device_id_type=MESH,
        ).wait_recv()

    barrier = pltpu.get_barrier_semaphore()
    peers = [zpeer(k) for k in range(1, 8)] + [right, left, yn, yp, xr, xp, x2, x2o, cp]
    for dev in peers:
        pl.semaphore_signal(barrier, inc=1, device_id=dev, device_id_type=MESH)
    pl.semaphore_wait(barrier, len(peers))

    def unit(j):
        return mod(y + j, 4) * 2 + xl

    def other(j):
        return mod(y + j, 4) * 2 + 1 - xl

    def part(u, p, h):
        return wf.at[pl.ds(8 * u + 4 * p, 4), h]

    def x_dev(p):
        return xr if p == 0 else xp

    def spread(j, p):
        ref = part(unit(j), p, c)
        send(f"x{j}{p}", ref, ref, x_dev(p))
        send(f"d{j}{p}", ref, ref, cp)

    def gather_z():
        for k in range(1, 8):
            send(f"z{k}", w_ref.at[c], wf.at[pos, c], zpeer(k))
        wf[pos, c] = w_ref[c]

    def gather_y():
        for k in range(1, 8):
            recv(f"z{k}", wf.at[pos - z + mod(z + 8 - k, 8), c])
        for p in range(2):
            ref = part(unit(0), p, c)
            send(f"ya{p}", ref, ref, yn)
            send(f"yb{p}", ref, ref, yp)
        for p in range(2):
            spread(0, p)

    def gather_y0():
        recv("ya0", part(unit(3), 0, c))
        ref = part(unit(3), 0, c)
        send("yf0", ref, ref, yn)
        spread(3, 0)
        recv("yb0", part(unit(1), 0, c))
        spread(1, 0)

    def gather_y1():
        recv("yb1", part(unit(1), 1, c))
        ref = part(unit(1), 1, c)
        send("yf1", ref, ref, yp)
        spread(1, 1)
        recv("ya1", part(unit(3), 1, c))
        spread(3, 1)

    def gather_y2():
        for p in range(2):
            recv(f"yf{p}", part(unit(2), p, c))
            spread(2, p)

    def gather_x(j):
        for p in range(2):
            ref = part(other(j), p, c)
            recv(f"x{j}{p}", ref)
            send(f"e{j}{p}", ref, ref, cp)

    def gather_done():
        for j in range(4):
            for p in range(2):
                recv(f"d{j}{p}", part(unit(j), p, oc))
                recv(f"e{j}{p}", part(other(j), p, oc))

    def halo_own(kh):
        send(f"ok{kh}", k_ref.at[:, col(kh)], k1.at[:, col(kh)], right)
        send(f"ov{kh}", v_ref.at[:, col(kh)], v1.at[:, col(kh)], right)

    def halo_relay(kh):
        recv(f"ok{kh}", k1.at[:, col(kh)])
        send(f"fk{kh}", k1.at[:, col(kh)], k2.at[:, col(kh)], right)
        recv(f"ov{kh}", v1.at[:, col(kh)])
        send(f"fv{kh}", v1.at[:, col(kh)], v2.at[:, col(kh)], right)

    def halo_last(kh):
        recv(f"fk{kh}", k2.at[:, col(kh)])
        recv(f"fv{kh}", v2.at[:, col(kh)])

    def lengths_send():
        send("l0", lt_ref, lts.at[0], cp)
        send("l1", lt_ref, lts.at[1], x2)
        send("l2", lt_ref, lts.at[2], x2o)

    def lengths():
        for n in range(3):
            recv(f"l{n}", lts.at[n])
        total = (lt_ref[...] + lts[0] + lts[1] + lts[2]).astype(F32)[0:1, 0:1]
        return SLOTS / total, lax.rsqrt(total)

    def masked():
        row = lax.broadcasted_iota(jnp.int32, (TOK, 1), 0)
        mk[...] = jnp.where(row < len_ref[0] - pos * TOK, og_ref[...], jnp.zeros((), BF16))

    def forward(h):
        kh = h // GROUP
        q = q_ref[:, col(h)]
        row = lax.broadcasted_iota(jnp.int32, (TOK, TOK), 0)
        cl = lax.broadcasted_iota(jnp.int32, (TOK, TOK), 1)
        far = jnp.where(pos >= 2, 0, 2 * TOK)
        near = jnp.where(pos >= 1, 0, 2 * TOK)
        allowed = (cl - row > far, cl >= near, cl <= row)
        es, ws = [], []
        total = jnp.zeros((TOK, 1), F32)
        for b, ref in enumerate((k2, k1, k_ref)):
            t = jnp.tanh(dot_nt(q, ref[:, col(kh)]) * (SCALE / CAP))
            e = jnp.where(allowed[b], jnp.exp2(t * (CAP * LOG2E)), 0.0)
            total = total + jnp.sum(e, axis=1, keepdims=True)
            es.append(e)
            ws.append(e * (SCALE - SCALE * (t * t)))
        inv = 1.0 / total
        out = jnp.zeros((TOK, HD), F32)
        for b, ref in enumerate((v2, v1, v_ref)):
            p = (es[b] * inv).astype(BF16)
            pb[h, b] = p
            pw[h, b] = (ws[b] * inv).astype(BF16)
            out = out + dot_nn(p, ref[:, col(kh)])
        at[:, col(h)] = out.astype(BF16)

    def weight_part(h):
        tw[...] = dot_tn(at[:, col(h)], mk[...]).reshape(8, 2, 16, D_OUT)
        sdb[h] = tw[:, oc].astype(BF16)
        dwm[h] = tw[:, c]
        send(f"rd{h}", sdb.at[h], rdb.at[h], cp)

    def forward_pair(kh):
        for g in range(GROUP):
            forward(kh * GROUP + g)
            weight_part(kh * GROUP + g)

    def reduce_x(kh):
        for g in range(GROUP):
            h = kh * GROUP + g
            recv(f"rd{h}", rdb.at[h])
        u, o = kh * 2 + xl, kh * 2 + 1 - xl
        xsb[kh] = (dwm[o] + rdb[o].astype(F32)).astype(BF16)
        dwm[u] = dwm[u] + rdb[u].astype(F32)
        for p in range(2):
            send(f"rx{kh}{p}", xsb.at[kh, pl.ds(4 * p, 4)], xrb.at[kh, pl.ds(4 * p, 4)], x_dev(p))

    def reduce_x_done(kh):
        for p in range(2):
            recv(f"rx{kh}{p}", xrb.at[kh, pl.ds(4 * p, 4)])
        u = kh * 2 + xl
        dwm[u] = dwm[u] + xrb[kh].astype(F32)

    def mine(j, p):
        return dwm[unit(j), pl.ds(4 * p, 4)]

    def y_send(n, value, dev):
        ysb[n] = value.astype(BF16)
        send(f"r{n}", ysb.at[n], yrb.at[n], dev)

    def reduce_y():
        y_send(0, mine(2, 0), yn)
        y_send(1, mine(2, 1), yp)
        y_send(2, mine(1, 1), yn)
        y_send(3, mine(3, 0), yp)

    def reduce_y2():
        recv("r0", yrb.at[0])
        y_send(4, mine(1, 0) + yrb[0].astype(F32), yn)
        recv("r1", yrb.at[1])
        y_send(5, mine(3, 1) + yrb[1].astype(F32), yp)

    def reduce_z():
        for n in range(2, 6):
            recv(f"r{n}", yrb.at[n])
        u = unit(0)
        lo = mine(0, 0) + yrb[3].astype(F32) + yrb[4].astype(F32)
        hi = mine(0, 1) + yrb[2].astype(F32) + yrb[5].astype(F32)
        dwm[u, pl.ds(0, 4)] = lo
        dwm[u, pl.ds(4, 4)] = hi
        zsb[pl.ds(0, 4)] = lo.astype(BF16)
        zsb[pl.ds(4, 4)] = hi.astype(BF16)
        for k in range(1, 8):
            send(f"rz{k}", zsb.at[mod(z + k, 8)], zrb.at[k], zpeer(k))

    def reduce_dp():
        total = dwm[unit(0), z]
        for k in range(1, 8):
            recv(f"rz{k}", zrb.at[k])
            total = total + zrb[k].astype(F32)
        fsb[...] = total.astype(BF16)
        send("f", fsb, frb, x2)

    def reduce_swap(weight_scale):
        recv("f", frb)
        total = (fsb[...].astype(F32) + frb[...].astype(F32)) * weight_scale
        hsb[...] = total
        send("h", hsb, hrb, cp)
        dw_ref[c] = total
        square = total * total * 0.5
        acc = sq_ref[...]
        for n in range(D_OUT // HD):
            acc = acc + square[0:8, n * HD : (n + 1) * HD] + square[8:16, n * HD : (n + 1) * HD]
        sq_ref[...] = acc

    def reduce_end():
        recv("h", hrb)
        dw_ref[oc] = hrb[...]

    def squares(x):
        sq_ref[...] += jnp.sum((x * x).reshape(TOK // 8, 8, HD), axis=0)

    def backward(kh, act_scale):
        sk = [None] * 3
        sv = [None] * 3
        for g in range(GROUP):
            h = kh * GROUP + g
            q = q_ref[:, col(h)]
            wh = wf[pl.ds(8 * h, 8)].reshape(HD, D_OUT)
            ga = dot_nt(mk[...], wh).astype(BF16)
            delta = jnp.sum(ga.astype(F32) * at[:, col(h)].astype(F32), axis=1, keepdims=True)
            dq = jnp.zeros((TOK, HD), F32)
            for b, (kr, vr) in enumerate(((k2, v2), (k1, v1), (k_ref, v_ref))):
                dp = dot_nt(ga, vr[:, col(kh)])
                ds = (pw[h, b].astype(F32) * (dp - delta)).astype(BF16)
                dq = dq + dot_nn(ds, kr[:, col(kh)])
                dk = dot_tn(ds, q)
                dv = dot_tn(pb[h, b], ga)
                sk[b] = dk if g == 0 else sk[b] + dk
                sv[b] = dv if g == 0 else sv[b] + dv
            dq = dq * act_scale
            squares(dq)
            dq_ref[:, col(h)] = dq.astype(BF16)
        c2s[kh, 0] = sk[0].astype(BF16)
        c2s[kh, 1] = sv[0].astype(BF16)
        send(f"b{kh}", c2s.at[kh], c2r.at[kh], left)
        c1[kh, 0] = sk[1]
        c1[kh, 1] = sv[1]
        c0[kh, 0] = sk[2]
        c0[kh, 1] = sv[2]

    def combine(kh):
        recv(f"b{kh}", c2r.at[kh])
        cms[kh] = (c1[kh] + c2r[kh].astype(F32)).astype(BF16)
        send(f"m{kh}", cms.at[kh], cmr.at[kh], left)

    def finish(kh, act_scale):
        recv(f"m{kh}", cmr.at[kh])
        for n, ref in enumerate((dk_ref, dv_ref)):
            total = (c0[kh, n] + cmr[kh, n].astype(F32)) * act_scale
            squares(total)
            ref[:, col(kh)] = total.astype(BF16)

    sq_ref[...] = jnp.zeros_like(sq_ref)
    gather_z()
    lengths_send()
    halo_own(0)
    halo_own(1)
    masked()
    gather_y()
    act_scale, weight_scale = lengths()
    halo_relay(0)
    halo_own(2)
    gather_y0()
    gather_y1()
    halo_last(0)
    forward_pair(0)
    gather_y2()
    halo_relay(1)
    halo_own(3)
    for j in (0, 1, 3, 2):
        gather_x(j)
    reduce_x(0)
    gather_done()
    backward(0, act_scale)
    halo_last(1)
    forward_pair(1)
    halo_relay(2)
    backward(1, act_scale)
    combine(0)
    halo_last(2)
    reduce_x_done(0)
    reduce_x(1)
    forward_pair(2)
    halo_relay(3)
    backward(2, act_scale)
    combine(1)
    finish(0, act_scale)
    reduce_x_done(1)
    reduce_x(2)
    halo_last(3)
    forward_pair(3)
    reduce_x_done(2)
    reduce_x(3)
    backward(3, act_scale)
    combine(2)
    finish(1, act_scale)
    reduce_x_done(3)
    reduce_y()
    reduce_y2()
    combine(3)
    finish(2, act_scale)
    reduce_z()
    reduce_dp()
    reduce_swap(weight_scale)
    finish(3, act_scale)
    reduce_end()
    for d in sent:
        d.wait_send()


def shards(queries, keys, values, out_grad, out_weight, seq_len):
    vm = pl.BlockSpec(memory_space=pltpu.VMEM)
    scratch = [
        ((64, 2, 16, D_OUT), BF16),
        ((TOK, 1024), BF16),
        ((TOK, 1024), BF16),
        ((TOK, 1024), BF16),
        ((TOK, 1024), BF16),
        ((TOK, D_OUT), BF16),
        ((TOK, 2048), BF16),
        ((HEADS, 3, TOK, TOK), BF16),
        ((HEADS, 3, TOK, TOK), BF16),
        ((8, 2, 16, D_OUT), F32),
        ((HEADS, 8, 16, D_OUT), F32),
        ((HEADS, 8, 16, D_OUT), BF16),
        ((HEADS, 8, 16, D_OUT), BF16),
        ((KV_HEADS, 8, 16, D_OUT), BF16),
        ((KV_HEADS, 8, 16, D_OUT), BF16),
        ((6, 4, 16, D_OUT), BF16),
        ((6, 4, 16, D_OUT), BF16),
        ((8, 16, D_OUT), BF16),
        ((8, 16, D_OUT), BF16),
        ((16, D_OUT), BF16),
        ((16, D_OUT), BF16),
        ((16, D_OUT), F32),
        ((16, D_OUT), F32),
        ((KV_HEADS, 2, TOK, HD), BF16),
        ((KV_HEADS, 2, TOK, HD), BF16),
        ((KV_HEADS, 2, TOK, HD), BF16),
        ((KV_HEADS, 2, TOK, HD), BF16),
        ((KV_HEADS, 2, TOK, HD), F32),
        ((KV_HEADS, 2, TOK, HD), F32),
        ((3, 8, 128), jnp.int32),
    ]
    dq, dk, dv, dw, sq = pl.pallas_call(
        body,
        out_shape=(
            jax.ShapeDtypeStruct((TOK, 2048), BF16),
            jax.ShapeDtypeStruct((TOK, 1024), BF16),
            jax.ShapeDtypeStruct((TOK, 1024), BF16),
            jax.ShapeDtypeStruct((2, 16, D_OUT), F32),
            jax.ShapeDtypeStruct((8, HD), F32),
        ),
        in_specs=[pl.BlockSpec(memory_space=pltpu.SMEM)] + [vm] * 6,
        out_specs=[vm] * 5,
        scratch_shapes=[pltpu.VMEM(s, d) for s, d in scratch]
        + [pltpu.SemaphoreType.DMA((CHANNELS,)), pltpu.SemaphoreType.DMA((CHANNELS,))],
        compiler_params=pltpu.CompilerParams(
            collective_id=0, has_side_effects=True, vmem_limit_bytes=67043328
        ),
        name="band",
    )(
        seq_len,
        queries[0],
        keys[0],
        values[0],
        out_grad[0],
        out_weight.reshape(2, 16, D_OUT),
        jnp.full((8, 128), seq_len[0], jnp.int32),
    )
    entries = SLOTS * (HEADS + 2 * KV_HEADS) * HD + HEADS * HD * D_OUT
    grad_rms = jnp.sqrt(lax.psum(jnp.sum(sq), AXES) / entries)
    return dq[None], dk[None], dv[None], dw.reshape(32, D_OUT), grad_rms


def solution(mesh):
    split = Mesh(mesh.devices.reshape(4, 2, 8, 2, 2), AXES)
    rows = P(DP, SEQ, None)
    return jax.shard_map(
        shards,
        mesh=split,
        in_specs=(rows, rows, rows, rows, P(SEQ, None), P(DP)),
        out_specs=(rows, rows, rows, P(SEQ, None), P()),
        check_vma=False,
    )
```

time: 784 us -> 272 us (0.35)
  waiting for transfers between devices: 549 us -> 0 us
  Pallas kernels: 0 us -> 185 us
  starting transfers between devices: 78.9 us -> 0 us
  matrix products: 37.8 us -> 0 us
  blocking collectives: 39.8 us -> 75.9 us
  local copies, waits for them, and re-layouts: 37.5 us -> 6 us
  between operations: 21.5 us -> 3.12 us
  other arithmetic: 18.2 us -> 1.3 us
    reduce_scatter x1 -> x0, waiting for transfers between devices: 302 us -> none  [shards(): lax.psum_scatter(lax.dot_general(attn, masked, (((0,), (0,)), ((), ())),...]
    all_gather x1 -> x0, waiting for transfers between devices: 195 us -> none  [shards(): lax.all_gather(out_weight, SEQ, axis=0, tiled=True)]
    pallas_call x0 -> x1, Pallas kernels: none -> 185 us  [shards(): pl.pallas_call(body, out_shape=(jax.ShapeDtypeStruct((TOK, 2048), BF16),...]
    all_to_all x1 -> x0, starting transfers between devices: 55.7 us -> none  [copy_for_each(): lax.all_to_all(jnp.broadcast_to(value[None], (size, *value.shape)), axis,...]
    ppermute x8 -> x0, waiting for transfers between devices: 48.6 us -> none  [shifted(): lax.ppermute(value, axis, [(source, source + steps) for source in range(i...]
    dot_general x8 -> x0, matrix products: 37.8 us -> none  [the longest x1 7.37 us: shards(): lax.dot_general(attn, masked, (((0,), (0,)), ((), ())), preferred_element...]
    psum x5 -> x1, blocking collectives: 39.8 us -> 75.9 us  [shards(): grad_rms = jnp.sqrt(lax.psum(jnp.sum(sq), AXES) / entries)]
    ppermute x8 -> x0, starting transfers between devices: 23.1 us -> none  [shifted(): lax.ppermute(value, axis, [(source, source + steps) for source in range(i...]
  transfers between devices with their start and end apart: 11 -> 0, of which waited for: 6 -> 0; matrix products, arithmetic and copies ran while one was open for 7% -> 0% of each run, Pallas kernels for 0% -> 0%
where the time goes in v1:
time: 272 us; the launch traced here: 271 us
  Pallas kernels  185 us (68%)
  blocking collectives  75.9 us (28%)
  local copies, waits for them, and re-layouts  6 us (2%)
  between operations  3.12 us (1%)
    pallas_call x1, Pallas kernels, shards(): pl.pallas_call(body, out_shape=(jax.ShapeDtypeStruct((TOK, 2048), BF16),...  185 us
    psum x1, blocking collectives, shards(): grad_rms = jnp.sqrt(lax.psum(jnp.sum(sq), AXES) / entries)  75.9 us

profile of v1, /device:TPU:1, one launch (start us, length us, event | category | flops | bytes accessed | tf_op | source)
XLA Modules:
  0.0 271.4 jit_solution(15121752838071864865)
XLA Ops:
  1.3 0.6 broadcast_in_dim.12.lt_ref
  1.9 185.1 %band.1 = (bf16[256,2048]{1,0:T(8,128)(2,1)}, bf16[256,1024]{1,0:T(8,128)(2,1)}, bf16[256,1024]{1,0:T(8,128)(2,1)}, f32[2,16,1792]{2,1,0:T(8,128)}, f32[8,256]{1,0:T(8,128)}) custom-call(s32[1]{0:T(128)} %copy.15.len_ref, bf16[256,2048]{1,0:T(8,128)(2,1)} %bitcast.12, bf16[256,1024]{1,0:T(8,128)(2,1)} %bitcast.16, bf16[256,1024]{1,0:T(8,128)(2,1)} %bitcast.17, ...), custom_call_target="tpu_custom_call" | custom-call | tf_op jit(solution)/shard_map/band/pallas_call | solution.py:445
  187.0 1.3 reduce_sum.9
  188.3 75.9 %psum.7 = f32[]{:T(128)} all-reduce(f32[]{:T(128)} %reduce_sum.9), channel_id=1, replica_groups=mesh['sy'=4,'sx'=2,'sz'=8,'dx'=2,'dc'=2] {'sy','sx','sz','dx','dc'}, use_global_device_ids=true, to_apply=%region_1.0 | all-reduce | flops 1 | bytes 8 | tf_op jit(solution)/shard_map/psum | solution.py:472
  264.9 0.0 copy-start.1
  264.9 2.4 copy.16
  267.2 0.0 copy-done.1
  267.2 0.0 copy-start
  267.2 0.8 copy.17
  268.0 0.4 copy-done
  268.5 0.0 copy-start.2
  268.5 0.8 copy.18
  269.3 0.3 copy-done.2
  269.6 0.7 copy.19
Async XLA Ops:
  264.9 2.4 copy-start.1
  267.2 1.2 copy-start
  268.5 1.1 copy-start.2

commit v2 on v1

--- a/solution.py
+++ b/solution.py
@@ -1,5 +1,3 @@
-import functools
-
 import jax
 import jax.numpy as jnp
 from jax import lax
@@ -24,7 +22,7 @@
 SCALE = 0.0625
 CAP = 50.0
 LOG2E = 1.4426950408889634
-CHANNELS = 128
+CHANNELS = 144
 
 F32 = jnp.float32
 BF16 = jnp.bfloat16
@@ -49,9 +47,9 @@
 
 def body(
     len_ref, q_ref, k_ref, v_ref, og_ref, w_ref, lt_ref,
-    dq_ref, dk_ref, dv_ref, dw_ref, sq_ref,
-    wf, k1, k2, v1, v2, mk, at, pb, pw, tw, dwm, sdb, rdb, xsb, xrb, ysb, yrb, zsb, zrb,
-    fsb, frb, hsb, hrb, c2s, c2r, cms, cmr, c1, c0, lts, ssem, rsem,
+    dq_ref, dk_ref, dv_ref, dw_ref, rms_ref,
+    sq_ref, wf, k1, k2, v1, v2, mk, at, pb, pw, tw, dwm, sdb, rdb, xsb, xrb, ysb, yrb, zsb, zrb,
+    fsb, frb, hsb, hrb, c2s, c2r, cms, cmr, c1, c0, lts, tz, ty, tx, ssem, rsem,
 ):
     y, xl, z, xh, c = (lax.axis_index(a) for a in AXES)
     oc = 1 - c
@@ -77,7 +75,7 @@
         return (y, xl, mod(z + k, 8), xh, c)
 
     ids = {}
-    sent = []
+    sent = {}
 
     def channel(name):
         return ids.setdefault(name, len(ids))
@@ -89,7 +87,7 @@
             device_id=dev, device_id_type=MESH,
         )
         d.start()
-        sent.append(d)
+        sent[name] = (n, src)
 
     def recv(name, dst):
         n = channel(name)
@@ -99,7 +97,11 @@
         ).wait_recv()
 
     barrier = pltpu.get_barrier_semaphore()
-    peers = [zpeer(k) for k in range(1, 8)] + [right, left, yn, yp, xr, xp, x2, x2o, cp]
+    yo = (mod(y + 2, 4), xl, z, xh, c)
+    xro = (*xr[:4], oc)
+    xpo = (*xp[:4], oc)
+    peers = [zpeer(k) for k in range(1, 8)]
+    peers += [right, left, yn, yp, yo, xr, xp, xro, xpo, x2, x2o, cp]
     for dev in peers:
         pl.semaphore_signal(barrier, inc=1, device_id=dev, device_id_type=MESH)
     pl.semaphore_wait(barrier, len(peers))
@@ -113,49 +115,93 @@
     def part(u, p, h):
         return wf.at[pl.ds(8 * u + 4 * p, 4), h]
 
-    def x_dev(p):
-        return xr if p == 0 else xp
+    ours = [[[part(unit(j), p, h) for h in (c, oc)] for p in range(2)] for j in range(4)]
+
+    first = 1 - lax.div(z + 7, 8)
+    last = lax.div(z, 7)
+    one_way = jnp.logical_and(z == 0, xl == 0)
+
+    def x_dev(p, outer):
+        near = mod(xh + xl, 2) if p == 0 else mod(xh + 1 - xl, 2)
+        return (y, 1 - xl, z, outer * (1 - xh) + (1 - outer) * near, c)
+
+    x_devs = [[x_dev(p, first if j in (1, 3) else 0) for p in range(2)] for j in range(4)]
 
     def spread(j, p):
-        ref = part(unit(j), p, c)
-        send(f"x{j}{p}", ref, ref, x_dev(p))
+        ref = ours[j][p][0]
+        send(f"x{j}{p}", ref, ref, x_devs[j][p])
         send(f"d{j}{p}", ref, ref, cp)
 
     def gather_z():
-        for k in range(1, 8):
-            send(f"z{k}", w_ref.at[c], wf.at[pos, c], zpeer(k))
-        wf[pos, c] = w_ref[c]
-
-    def gather_y():
-        for k in range(1, 8):
-            recv(f"z{k}", wf.at[pos - z + mod(z + 8 - k, 8), c])
-        for p in range(2):
-            ref = part(unit(0), p, c)
+        for k in (1, 7, 6, 2, 3, 5, 4):
+            send(f"z{k}", w_ref.at[c], wf.at[pos - z + (9 - k) % 8, c], zpeer(k))
+        wf[pos - z + 1, c] = w_ref[c]
+
+    def gather_y(p):
+        for k in ((1, 7, 6), (2, 3, 5, 4))[p]:
+            recv(f"z{k}", wf.at[pos - z + (9 - k) % 8, c])
+        ref = ours[0][p][0]
+
+        @pl.when(jnp.logical_not(one_way))
+        def _():
             send(f"ya{p}", ref, ref, yn)
-            send(f"yb{p}", ref, ref, yp)
-        for p in range(2):
-            spread(0, p)
+
+        send(f"yb{p}", ref, ref, yp)
+        spread(0, p)
+
+    def gather_ya(p):
+        ref = ours[3][p][0]
+        recv(f"ya{p}", ref)
+        if p == 0:
+
+            @pl.when(jnp.logical_not(one_way))
+            def _():
+                send("yf0", ref, ref, yn)
+
+        spread(3, p)
+
+    def gather_yb(p):
+        ref = ours[1][p][0]
+        recv(f"yb{p}", ref)
+        if p == 0:
+
+            @pl.when(one_way)
+            def _():
+                send("yf0", ref, ref, yp)
+
+        else:
+            send("yf1", ref, ref, yp)
+        spread(1, p)
 
     def gather_y0():
-        recv("ya0", part(unit(3), 0, c))
-        ref = part(unit(3), 0, c)
-        send("yf0", ref, ref, yn)
-        spread(3, 0)
-        recv("yb0", part(unit(1), 0, c))
-        spread(1, 0)
+        @pl.when(jnp.logical_not(one_way))
+        def _():
+            gather_ya(0)
+
+        gather_yb(0)
 
     def gather_y1():
-        recv("yb1", part(unit(1), 1, c))
-        ref = part(unit(1), 1, c)
-        send("yf1", ref, ref, yp)
-        spread(1, 1)
-        recv("ya1", part(unit(3), 1, c))
-        spread(3, 1)
-
-    def gather_y2():
-        for p in range(2):
-            recv(f"yf{p}", part(unit(2), p, c))
-            spread(2, p)
+        gather_yb(1)
+
+        @pl.when(jnp.logical_not(one_way))
+        def _():
+            gather_ya(1)
+
+    def gather_y2(p):
+        ref = ours[2][p][0]
+        recv(f"yf{p}", ref)
+
+        @pl.when(one_way)
+        def _():
+            send(f"ya{p}", ref, ref, yp)
+
+        spread(2, p)
+
+    def gather_y3():
+        @pl.when(one_way)
+        def _():
+            for p in range(2):
+                gather_ya(p)
 
     def gather_x(j):
         for p in range(2):
@@ -166,8 +212,14 @@
     def gather_done():
         for j in range(4):
             for p in range(2):
-                recv(f"d{j}{p}", part(unit(j), p, oc))
+                recv(f"d{j}{p}", ours[j][p][1])
                 recv(f"e{j}{p}", part(other(j), p, oc))
+
+    def unless_last(fn):
+        pl.when(z != 7)(fn)
+
+    def if_last(fn):
+        pl.when(z == 7)(fn)
 
     def halo_own(kh):
         send(f"ok{kh}", k_ref.at[:, col(kh)], k1.at[:, col(kh)], right)
@@ -238,11 +290,12 @@
         for g in range(GROUP):
             h = kh * GROUP + g
             recv(f"rd{h}", rdb.at[h])
+        outer = last if kh == 3 else first + last
         u, o = kh * 2 + xl, kh * 2 + 1 - xl
         xsb[kh] = (dwm[o] + rdb[o].astype(F32)).astype(BF16)
         dwm[u] = dwm[u] + rdb[u].astype(F32)
         for p in range(2):
-            send(f"rx{kh}{p}", xsb.at[kh, pl.ds(4 * p, 4)], xrb.at[kh, pl.ds(4 * p, 4)], x_dev(p))
+            send(f"rx{kh}{p}", xsb.at[kh, pl.ds(4 * p, 4)], xrb.at[kh, pl.ds(4 * p, 4)], x_dev(p, outer))
 
     def reduce_x_done(kh):
         for p in range(2):
@@ -250,37 +303,59 @@
         u = kh * 2 + xl
         dwm[u] = dwm[u] + xrb[kh].astype(F32)
 
-    def mine(j, p):
-        return dwm[unit(j), pl.ds(4 * p, 4)]
+    def mine(kh, p):
+        return dwm[kh * 2 + xl, pl.ds(4 * p, 4)]
+
+    y_refs = [ysb.at[n] for n in range(6)]
 
     def y_send(n, value, dev):
         ysb[n] = value.astype(BF16)
-        send(f"r{n}", ysb.at[n], yrb.at[n], dev)
-
-    def reduce_y():
-        y_send(0, mine(2, 0), yn)
-        y_send(1, mine(2, 1), yp)
-        y_send(2, mine(1, 1), yn)
-        y_send(3, mine(3, 0), yp)
-
-    def reduce_y2():
-        recv("r0", yrb.at[0])
-        y_send(4, mine(1, 0) + yrb[0].astype(F32), yn)
-        recv("r1", yrb.at[1])
-        y_send(5, mine(3, 1) + yrb[1].astype(F32), yp)
-
-    def reduce_z():
-        for n in range(2, 6):
-            recv(f"r{n}", yrb.at[n])
-        u = unit(0)
-        lo = mine(0, 0) + yrb[3].astype(F32) + yrb[4].astype(F32)
-        hi = mine(0, 1) + yrb[2].astype(F32) + yrb[5].astype(F32)
-        dwm[u, pl.ds(0, 4)] = lo
-        dwm[u, pl.ds(4, 4)] = hi
-        zsb[pl.ds(0, 4)] = lo.astype(BF16)
-        zsb[pl.ds(4, 4)] = hi.astype(BF16)
-        for k in range(1, 8):
-            send(f"rz{k}", zsb.at[mod(z + k, 8)], zrb.at[k], zpeer(k))
+        send(f"r{n}", y_refs[n], yrb.at[n], dev)
+
+    def role(kh, j):
+        return pl.when(mod(kh - y + 4, 4) == j)
+
+    def reduce_y(kh):
+        @role(kh, 2)
+        def _():
+            y_send(0, mine(kh, 0), yn)
+            y_send(1, mine(kh, 1), yp)
+
+        @role(kh, 1)
+        def _():
+            y_send(2, mine(kh, 1), yn)
+
+        @role(kh, 3)
+        def _():
+            y_send(3, mine(kh, 0), yp)
+
+    def reduce_y2(kh):
+        @role(kh, 1)
+        def _():
+            recv("r0", yrb.at[0])
+            y_send(4, mine(kh, 0) + yrb[0].astype(F32), yn)
+
+        @role(kh, 3)
+        def _():
+            recv("r1", yrb.at[1])
+            y_send(5, mine(kh, 1) + yrb[1].astype(F32), yp)
+
+    z_refs = [zsb.at[mod(z + k, 8)] for k in range(8)]
+
+    def reduce_z(kh):
+        @role(kh, 0)
+        def _():
+            for n in range(2, 6):
+                recv(f"r{n}", yrb.at[n])
+            u = kh * 2 + xl
+            lo = mine(kh, 0) + yrb[3].astype(F32) + yrb[4].astype(F32)
+            hi = mine(kh, 1) + yrb[2].astype(F32) + yrb[5].astype(F32)
+            dwm[u, pl.ds(0, 4)] = lo
+            dwm[u, pl.ds(4, 4)] = hi
+            zsb[pl.ds(0, 4)] = lo.astype(BF16)
+            zsb[pl.ds(4, 4)] = hi.astype(BF16)
+            for k in range(1, 8):
+                send(f"rz{k}", z_refs[k], zrb.at[k], zpeer(k))
 
     def reduce_dp():
         total = dwm[unit(0), z]
@@ -315,7 +390,8 @@
         for g in range(GROUP):
             h = kh * GROUP + g
             q = q_ref[:, col(h)]
-            wh = wf[pl.ds(8 * h, 8)].reshape(HD, D_OUT)
+            blocks = [wf[8 * h + mod(n + 9 - z, 8)].reshape(32, D_OUT) for n in range(8)]
+            wh = jnp.concatenate(blocks, axis=0)
             ga = dot_nt(mk[...], wh).astype(BF16)
             delta = jnp.sum(ga.astype(F32) * at[:, col(h)].astype(F32), axis=1, keepdims=True)
             dq = jnp.zeros((TOK, HD), F32)
@@ -350,67 +426,187 @@
             squares(total)
             ref[:, col(kh)] = total.astype(BF16)
 
+    def everyone(name, buf, at_me, value, devs):
+        buf[at_me] = value
+        for n, dev in enumerate(devs):
+            send(f"{name}{n}", buf.at[at_me], buf.at[at_me], dev)
+
+    def heard(name, buf, slots):
+        for n, slot in enumerate(slots):
+            recv(f"{name}{n}", buf.at[slot])
+        total = buf[0]
+        for n in range(1, buf.shape[0]):
+            total = total + buf[n]
+        return total
+
+    def rms():
+        own = jnp.sum(jnp.sum(sq_ref[...], axis=0, keepdims=True), axis=1, keepdims=True)
+        own = jnp.broadcast_to(own, (8, 128))
+        everyone("sz", tz, z, own, [zpeer(k) for k in range(1, 8)])
+        total = heard("sz", tz, [mod(z + 8 - k, 8) for k in range(1, 8)])
+        everyone("sy", ty, y, total, [yn, yp, yo])
+        total = heard("sy", ty, [mod(y + 3, 4), mod(y + 1, 4), mod(y + 2, 4)])
+        x = xh * 2 + xl
+        up, down, far = mod(x + 1, 4), mod(x + 3, 4), mod(x + 2, 4)
+        everyone("sx", tx, x * 2 + c, total, [xr, xp, x2, xro, xpo, x2o, cp])
+        slots = [down * 2 + c, up * 2 + c, far * 2 + c]
+        slots += [down * 2 + oc, up * 2 + oc, far * 2 + oc, x * 2 + oc]
+        total = heard("sx", tx, slots)
+        entries = SLOTS * (HEADS + 2 * KV_HEADS) * HD + HEADS * HD * D_OUT
+        rms_ref[...] = jnp.sqrt(total * (1.0 / entries))
+
     sq_ref[...] = jnp.zeros_like(sq_ref)
-    gather_z()
-    lengths_send()
-    halo_own(0)
-    halo_own(1)
-    masked()
-    gather_y()
-    act_scale, weight_scale = lengths()
-    halo_relay(0)
-    halo_own(2)
-    gather_y0()
-    gather_y1()
-    halo_last(0)
-    forward_pair(0)
-    gather_y2()
-    halo_relay(1)
-    halo_own(3)
-    for j in (0, 1, 3, 2):
-        gather_x(j)
-    reduce_x(0)
-    gather_done()
-    backward(0, act_scale)
-    halo_last(1)
-    forward_pair(1)
-    halo_relay(2)
-    backward(1, act_scale)
-    combine(0)
-    halo_last(2)
-    reduce_x_done(0)
-    reduce_x(1)
-    forward_pair(2)
-    halo_relay(3)
-    backward(2, act_scale)
-    combine(1)
-    finish(0, act_scale)
-    reduce_x_done(1)
-    reduce_x(2)
-    halo_last(3)
-    forward_pair(3)
-    reduce_x_done(2)
-    reduce_x(3)
-    backward(3, act_scale)
-    combine(2)
-    finish(1, act_scale)
-    reduce_x_done(3)
-    reduce_y()
-    reduce_y2()
-    combine(3)
-    finish(2, act_scale)
-    reduce_z()
-    reduce_dp()
-    reduce_swap(weight_scale)
-    finish(3, act_scale)
-    reduce_end()
-    for d in sent:
-        d.wait_send()
+    with jax.named_scope("gather_z"):
+        gather_z()
+    with jax.named_scope("lengths_send"):
+        lengths_send()
+    with jax.named_scope("halo_own#0"):
+        halo_own(0)
+    with jax.named_scope("masked"):
+        masked()
+    with jax.named_scope("gather_y#0"):
+        gather_y(0)
+    with jax.named_scope("lengths"):
+        act_scale, weight_scale = lengths()
+    with jax.named_scope("gather_y#1"):
+        gather_y(1)
+    with jax.named_scope("gather_y0"):
+        gather_y0()
+    with jax.named_scope("halo_relay#0"):
+        halo_relay(0)
+    with jax.named_scope("halo_own#1"):
+        unless_last(lambda: halo_own(1))
+    with jax.named_scope("gather_y1"):
+        gather_y1()
+    with jax.named_scope("gather_y2#0"):
+        gather_y2(0)
+    with jax.named_scope("gather_y2#1"):
+        gather_y2(1)
+    with jax.named_scope("gather_y3"):
+        gather_y3()
+    with jax.named_scope("halo_last#0"):
+        halo_last(0)
+    with jax.named_scope("forward_pair#0"):
+        forward_pair(0)
+    with jax.named_scope("halo_relay#1"):
+        pl.when(first + last == 0)(lambda: [halo_relay(1), halo_own(2)] and None)
+        pl.when(first == 1)(lambda: halo_own(2))
+    with jax.named_scope("gather_x#0"):
+        gather_x(0)
+    with jax.named_scope("gather_x#1"):
+        gather_x(1)
+    with jax.named_scope("gather_x#3"):
+        gather_x(3)
+    with jax.named_scope("gather_x#2"):
+        gather_x(2)
+    with jax.named_scope("reduce_x#0"):
+        reduce_x(0)
+    with jax.named_scope("gather_done"):
+        gather_done()
+    with jax.named_scope("halo_late#1"):
+        if_last(lambda: [halo_own(1), halo_relay(1), halo_own(2)] and None)
+    with jax.named_scope("backward#0"):
+        backward(0, act_scale)
+    with jax.named_scope("halo_late#0"):
+        pl.when(first == 1)(lambda: halo_relay(1))
+    with jax.named_scope("halo_relay#2"):
+        halo_relay(2)
+    with jax.named_scope("halo_own#3"):
+        halo_own(3)
+    with jax.named_scope("halo_last#1"):
+        halo_last(1)
+    with jax.named_scope("forward_pair#1"):
+        forward_pair(1)
+    with jax.named_scope("reduce_x_done#0"):
+        reduce_x_done(0)
+    with jax.named_scope("reduce_y#0"):
+        reduce_y(0)
+    with jax.named_scope("reduce_x#1"):
+        reduce_x(1)
+    with jax.named_scope("backward#1"):
+        backward(1, act_scale)
+    with jax.named_scope("combine#0"):
+        combine(0)
+    with jax.named_scope("halo_relay#3"):
+        halo_relay(3)
+    with jax.named_scope("halo_last#2"):
+        halo_last(2)
+    with jax.named_scope("forward_pair#2"):
+        forward_pair(2)
+    with jax.named_scope("reduce_y2#0"):
+        reduce_y2(0)
+    with jax.named_scope("reduce_x_done#1"):
+        reduce_x_done(1)
+    with jax.named_scope("reduce_y#1"):
+        reduce_y(1)
+    with jax.named_scope("reduce_x#2"):
+        reduce_x(2)
+    with jax.named_scope("backward#2"):
+        backward(2, act_scale)
+    with jax.named_scope("combine#1"):
+        combine(1)
+    with jax.named_scope("halo_last#3"):
+        halo_last(3)
+    with jax.named_scope("forward_pair#3"):
+        forward_pair(3)
+    with jax.named_scope("reduce_z#0"):
+        reduce_z(0)
+    with jax.named_scope("reduce_y2#1"):
+        reduce_y2(1)
+    with jax.named_scope("reduce_x_done#2"):
+        reduce_x_done(2)
+    with jax.named_scope("reduce_y#2"):
+        reduce_y(2)
+    with jax.named_scope("reduce_x#3"):
+        reduce_x(3)
+    with jax.named_scope("backward#3"):
+        backward(3, act_scale)
+    with jax.named_scope("combine#2"):
+        combine(2)
+    with jax.named_scope("finish#0"):
+        finish(0, act_scale)
+    with jax.named_scope("reduce_z#1"):
+        reduce_z(1)
+    with jax.named_scope("reduce_y2#2"):
+        reduce_y2(2)
+    with jax.named_scope("reduce_x_done#3"):
+        reduce_x_done(3)
+    with jax.named_scope("reduce_y#3"):
+        reduce_y(3)
+    with jax.named_scope("finish#1"):
+        finish(1, act_scale)
+    with jax.named_scope("reduce_z#2"):
+        reduce_z(2)
+    with jax.named_scope("combine#3"):
+        combine(3)
+    with jax.named_scope("reduce_y2#3"):
+        reduce_y2(3)
+    with jax.named_scope("finish#2"):
+        finish(2, act_scale)
+    with jax.named_scope("reduce_z#3"):
+        reduce_z(3)
+    with jax.named_scope("reduce_dp"):
+        reduce_dp()
+    with jax.named_scope("finish#3"):
+        finish(3, act_scale)
+    with jax.named_scope("reduce_swap"):
+        reduce_swap(weight_scale)
+    with jax.named_scope("rms"):
+        rms()
+    with jax.named_scope("reduce_end"):
+        reduce_end()
+    with jax.named_scope("drain"):
+        for n, src in sent.values():
+            pltpu.make_async_remote_copy(
+                src_ref=src, dst_ref=src, send_sem=ssem.at[n], recv_sem=rsem.at[n],
+                device_id=cp, device_id_type=MESH,
+            ).wait_send()
 
 
 def shards(queries, keys, values, out_grad, out_weight, seq_len):
     vm = pl.BlockSpec(memory_space=pltpu.VMEM)
     scratch = [
+        ((8, HD), F32),
         ((64, 2, 16, D_OUT), BF16),
         ((TOK, 1024), BF16),
         ((TOK, 1024), BF16),
@@ -441,15 +637,18 @@
         ((KV_HEADS, 2, TOK, HD), F32),
         ((KV_HEADS, 2, TOK, HD), F32),
         ((3, 8, 128), jnp.int32),
+        ((8, 8, 128), F32),
+        ((4, 8, 128), F32),
+        ((8, 8, 128), F32),
     ]
-    dq, dk, dv, dw, sq = pl.pallas_call(
+    dq, dk, dv, dw, rms = pl.pallas_call(
         body,
         out_shape=(
             jax.ShapeDtypeStruct((TOK, 2048), BF16),
             jax.ShapeDtypeStruct((TOK, 1024), BF16),
             jax.ShapeDtypeStruct((TOK, 1024), BF16),
             jax.ShapeDtypeStruct((2, 16, D_OUT), F32),
-            jax.ShapeDtypeStruct((8, HD), F32),
+            jax.ShapeDtypeStruct((8, 128), F32),
         ),
         in_specs=[pl.BlockSpec(memory_space=pltpu.SMEM)] + [vm] * 6,
         out_specs=[vm] * 5,
@@ -468,9 +667,7 @@
         out_weight.reshape(2, 16, D_OUT),
         jnp.full((8, 128), seq_len[0], jnp.int32),
     )
-    entries = SLOTS * (HEADS + 2 * KV_HEADS) * HD + HEADS * HD * D_OUT
-    grad_rms = jnp.sqrt(lax.psum(jnp.sum(sq), AXES) / entries)
-    return dq[None], dk[None], dv[None], dw.reshape(32, D_OUT), grad_rms
+    return dq[None], dk[None], dv[None], dw.reshape(32, D_OUT), rms[0, 0]
 
 
 def solution(mesh):

time: 272 us -> 171 us (0.63)
  blocking collectives: 75.9 us -> 0 us
  Pallas kernels: 185 us -> 162 us
    psum x1 -> x0, blocking collectives: 75.9 us -> none  [shards(): grad_rms = jnp.sqrt(lax.psum(jnp.sum(sq), AXES) / entries)]
    pallas_call x1, Pallas kernels: 185 us -> 162 us  [shards(): pl.pallas_call(body, out_shape=(jax.ShapeDtypeStruct((TOK, 2048), BF16),...]
where the time goes in v2:
time: 171 us
  Pallas kernels  162 us (95%)
  local copies, waits for them, and re-layouts  7.19 us (4%)
    pallas_call x1, Pallas kernels, shards(): pl.pallas_call(body, out_shape=(jax.ShapeDtypeStruct((TOK, 2048), BF16),...  162 us
    unnamed x10, local copies, waits for them, and re-layouts  5.41 us

profile of v2, /device:TPU:1, one launch (start us, length us, event | category | flops | bytes accessed | tf_op | source)
XLA Modules:
  0.0 170.6 jit_solution(17819789556963952665)
XLA Ops:
  1.3 0.6 broadcast_in_dim.12.lt_ref
  1.9 162.1 %band.1 = (bf16[256,2048]{1,0:T(8,128)(2,1)}, bf16[256,1024]{1,0:T(8,128)(2,1)}, bf16[256,1024]{1,0:T(8,128)(2,1)}, f32[2,16,1792]{2,1,0:T(8,128)}, f32[8,128]{1,0:T(8,128)}) custom-call(s32[1]{0:T(128)} %copy.15.len_ref, bf16[256,2048]{1,0:T(8,128)(2,1)} %bitcast.13, bf16[256,1024]{1,0:T(8,128)(2,1)} %bitcast.17, bf16[256,1024]{1,0:T(8,128)(2,1)} %bitcast.18, ...), custom_call_target="tpu_custom_call" | custom-call | tf_op jit(solution)/shard_map/band/pallas_call | solution.py:644
  164.0 1.2 slice.3
  165.2 0.0 copy-start.1
  165.2 2.4 %copy.16 = bf16[1,256,2048]{2,1,0:T(8,128)(2,1)} copy(bf16[1,256,2048]{2,1,0:T(8,128)(2,1)} %bitcast.12) | data formatting | bytes 2097152
  167.5 0.0 copy-done.1
  167.5 0.0 copy-start
  167.5 0.8 copy.17
  168.3 0.4 copy-done
  168.8 0.0 copy-start.2
  168.8 0.8 copy.18
  169.5 0.3 copy-done.2
  169.9 0.7 copy.19
Async XLA Ops:
  165.2 2.4 %copy-start.1 = (bf16[256,1024]{1,0:T(8,128)(2,1)S(1)}, bf16[256,1024]{1,0:T(8,128)(2,1)}, u32[]{:S(2)}) copy-start(bf16[256,1024]{1,0:T(8,128)(2,1)} %get-tuple-element.11) | copy-start | bytes 1572868
  167.5 1.2 copy-start
  168.8 1.1 copy-start.2

commit v3 on v2

--- a/solution.py
+++ b/solution.py
@@ -48,7 +48,7 @@
 def body(
     len_ref, q_ref, k_ref, v_ref, og_ref, w_ref, lt_ref,
     dq_ref, dk_ref, dv_ref, dw_ref, rms_ref,
-    sq_ref, wf, k1, k2, v1, v2, mk, at, pb, pw, tw, dwm, sdb, rdb, xsb, xrb, ysb, yrb, zsb, zrb,
+    sq_ref, wf, k1, k2, v1, v2, mk, mk2, at, at2, ga, gs, pb, pw, tw, dwm, sdb, rdb, ysb, yrb, zsb, zrb,
     fsb, frb, hsb, hrb, c2s, c2r, cms, cmr, c1, c0, lts, tz, ty, tx, ssem, rsem,
 ):
     y, xl, z, xh, c = (lax.axis_index(a) for a in AXES)
@@ -70,6 +70,7 @@
     x2 = (y, xl, z, 1 - xh, c)
     x2o = (y, xl, z, 1 - xh, oc)
     cp = (y, xl, z, xh, oc)
+    pair = (y, 1 - xl, z, 1 - xh, c)
 
     def zpeer(k):
         return (y, xl, mod(z + k, 8), xh, c)
@@ -107,119 +108,81 @@
     pl.semaphore_wait(barrier, len(peers))
 
     def unit(j):
-        return mod(y + j, 4) * 2 + xl
-
-    def other(j):
-        return mod(y + j, 4) * 2 + 1 - xl
+        return mod(y + j, 4)
 
     def part(u, p, h):
         return wf.at[pl.ds(8 * u + 4 * p, 4), h]
 
     ours = [[[part(unit(j), p, h) for h in (c, oc)] for p in range(2)] for j in range(4)]
 
-    first = 1 - lax.div(z + 7, 8)
-    last = lax.div(z, 7)
     one_way = jnp.logical_and(z == 0, xl == 0)
-
-    def x_dev(p, outer):
-        near = mod(xh + xl, 2) if p == 0 else mod(xh + 1 - xl, 2)
-        return (y, 1 - xl, z, outer * (1 - xh) + (1 - outer) * near, c)
-
-    x_devs = [[x_dev(p, first if j in (1, 3) else 0) for p in range(2)] for j in range(4)]
 
     def spread(j, p):
         ref = ours[j][p][0]
-        send(f"x{j}{p}", ref, ref, x_devs[j][p])
         send(f"d{j}{p}", ref, ref, cp)
 
     def gather_z():
         for k in (1, 7, 6, 2, 3, 5, 4):
-            send(f"z{k}", w_ref.at[c], wf.at[pos - z + (9 - k) % 8, c], zpeer(k))
-        wf[pos - z + 1, c] = w_ref[c]
+            send(f"z{k}", w_ref.at[c], wf.at[8 * y + (9 - k) % 8, c], zpeer(k))
+        wf[8 * y + 1, c] = w_ref[c]
 
     def gather_y(p):
         for k in ((1, 7, 6), (2, 3, 5, 4))[p]:
-            recv(f"z{k}", wf.at[pos - z + (9 - k) % 8, c])
+            recv(f"z{k}", wf.at[8 * y + (9 - k) % 8, c])
         ref = ours[0][p][0]
-
-        @pl.when(jnp.logical_not(one_way))
-        def _():
-            send(f"ya{p}", ref, ref, yn)
+        if p == 0:
+            send("ya0", ref, ref, yn)
+        else:
+
+            @pl.when(jnp.logical_not(one_way))
+            def _():
+                send("ya1", ref, ref, yn)
 
         send(f"yb{p}", ref, ref, yp)
         spread(0, p)
 
-    def gather_ya(p):
-        ref = ours[3][p][0]
-        recv(f"ya{p}", ref)
-        if p == 0:
-
-            @pl.when(jnp.logical_not(one_way))
-            def _():
-                send("yf0", ref, ref, yn)
-
-        spread(3, p)
-
-    def gather_yb(p):
-        ref = ours[1][p][0]
-        recv(f"yb{p}", ref)
-        if p == 0:
-
-            @pl.when(one_way)
-            def _():
-                send("yf0", ref, ref, yp)
-
-        else:
-            send("yf1", ref, ref, yp)
-        spread(1, p)
-
     def gather_y0():
+        ref = ours[3][0][0]
+        recv("ya0", ref)
+
         @pl.when(jnp.logical_not(one_way))
         def _():
-            gather_ya(0)
-
-        gather_yb(0)
+            send("yf0", ref, ref, yn)
+
+        spread(3, 0)
+        ref = ours[1][0][0]
+        recv("yb0", ref)
+
+        @pl.when(one_way)
+        def _():
+            send("yf0", ref, ref, yp)
+
+        spread(1, 0)
+
+    def gather_ya1():
+        recv("ya1", ours[3][1][0])
+        spread(3, 1)
 
     def gather_y1():
-        gather_yb(1)
-
-        @pl.when(jnp.logical_not(one_way))
-        def _():
-            gather_ya(1)
+        ref = ours[1][1][0]
+        recv("yb1", ref)
+        send("yf1", ref, ref, yp)
+        spread(1, 1)
+        pl.when(jnp.logical_not(one_way))(gather_ya1)
 
     def gather_y2(p):
         ref = ours[2][p][0]
         recv(f"yf{p}", ref)
-
-        @pl.when(one_way)
-        def _():
-            send(f"ya{p}", ref, ref, yp)
+        if p == 1:
+
+            @pl.when(one_way)
+            def _():
+                send("ya1", ref, ref, yp)
 
         spread(2, p)
 
     def gather_y3():
-        @pl.when(one_way)
-        def _():
-            for p in range(2):
-                gather_ya(p)
-
-    def gather_x(j):
-        for p in range(2):
-            ref = part(other(j), p, c)
-            recv(f"x{j}{p}", ref)
-            send(f"e{j}{p}", ref, ref, cp)
-
-    def gather_done():
-        for j in range(4):
-            for p in range(2):
-                recv(f"d{j}{p}", ours[j][p][1])
-                recv(f"e{j}{p}", part(other(j), p, oc))
-
-    def unless_last(fn):
-        pl.when(z != 7)(fn)
-
-    def if_last(fn):
-        pl.when(z == 7)(fn)
+        pl.when(one_way)(gather_ya1)
 
     def halo_own(kh):
         send(f"ok{kh}", k_ref.at[:, col(kh)], k1.at[:, col(kh)], right)
@@ -231,6 +194,12 @@
         recv(f"ov{kh}", v1.at[:, col(kh)])
         send(f"fv{kh}", v1.at[:, col(kh)], v2.at[:, col(kh)], right)
 
+    def relay_a():
+        pl.when(z < 7)(lambda: [halo_relay(0), halo_own(1)] and None)
+
+    def relay_b():
+        pl.when(z == 7)(lambda: [halo_relay(0), halo_own(1)] and None)
+
     def halo_last(kh):
         recv(f"fk{kh}", k2.at[:, col(kh)])
         recv(f"fv{kh}", v2.at[:, col(kh)])
@@ -249,6 +218,7 @@
     def masked():
         row = lax.broadcasted_iota(jnp.int32, (TOK, 1), 0)
         mk[...] = jnp.where(row < len_ref[0] - pos * TOK, og_ref[...], jnp.zeros((), BF16))
+        send("xm", mk, mk2, pair)
 
     def forward(h):
         kh = h // GROUP
@@ -273,38 +243,39 @@
             pb[h, b] = p
             pw[h, b] = (ws[b] * inv).astype(BF16)
             out = out + dot_nn(p, ref[:, col(kh)])
-        at[:, col(h)] = out.astype(BF16)
-
-    def weight_part(h):
-        tw[...] = dot_tn(at[:, col(h)], mk[...]).reshape(8, 2, 16, D_OUT)
-        sdb[h] = tw[:, oc].astype(BF16)
-        dwm[h] = tw[:, c]
-        send(f"rd{h}", sdb.at[h], rdb.at[h], cp)
+        at[h] = out.astype(BF16)
 
     def forward_pair(kh):
         for g in range(GROUP):
             forward(kh * GROUP + g)
-            weight_part(kh * GROUP + g)
-
-    def reduce_x(kh):
-        for g in range(GROUP):
-            h = kh * GROUP + g
-            recv(f"rd{h}", rdb.at[h])
-        outer = last if kh == 3 else first + last
-        u, o = kh * 2 + xl, kh * 2 + 1 - xl
-        xsb[kh] = (dwm[o] + rdb[o].astype(F32)).astype(BF16)
-        dwm[u] = dwm[u] + rdb[u].astype(F32)
-        for p in range(2):
-            send(f"rx{kh}{p}", xsb.at[kh, pl.ds(4 * p, 4)], xrb.at[kh, pl.ds(4 * p, 4)], x_dev(p, outer))
-
-    def reduce_x_done(kh):
-        for p in range(2):
-            recv(f"rx{kh}{p}", xrb.at[kh, pl.ds(4 * p, 4)])
-        u = kh * 2 + xl
-        dwm[u] = dwm[u] + xrb[kh].astype(F32)
+        send(f"xa{kh}", at.at[kh * GROUP + 1 - xl], at2.at[kh], pair)
+
+    def project(kh):
+        if kh == 0:
+            recv("xm", mk2)
+        for j in range(4):
+
+            @pl.when(mod(kh - y + 4, 4) == j)
+            def _():
+                for p in range(2):
+                    recv(f"d{j}{p}", ours[j][p][1])
+
+        blocks = [wf[8 * kh + mod(n + 9 - z, 8)].reshape(32, D_OUT) for n in range(8)]
+        wh = jnp.concatenate(blocks, axis=0)
+        gs[kh] = dot_nt(mk2[...], wh).astype(BF16)
+        send(f"xg{kh}", gs.at[kh], ga.at[kh, xl], pair)
+        ga[kh, xl] = dot_nt(mk[...], wh).astype(BF16)
+
+    def weight(kh):
+        recv(f"xa{kh}", at2.at[kh])
+        total = dot_tn(at[kh * GROUP + xl], mk[...]) + dot_tn(at2[kh], mk2[...])
+        tw[...] = total.reshape(8, 2, 16, D_OUT)
+        sdb[kh] = tw[:, oc].astype(BF16)
+        dwm[kh] = tw[:, c]
+        send(f"rd{kh}", sdb.at[kh], rdb.at[kh], cp)
 
     def mine(kh, p):
-        return dwm[kh * 2 + xl, pl.ds(4 * p, 4)]
+        return dwm[kh, pl.ds(4 * p, 4)]
 
     y_refs = [ysb.at[n] for n in range(6)]
 
@@ -315,50 +286,80 @@
     def role(kh, j):
         return pl.when(mod(kh - y + 4, 4) == j)
 
+    one = xl * lax.div(z, 7)
+
+    def role_if(kh, j, flag):
+        return pl.when(jnp.logical_and(mod(kh - y + 4, 4) == j, one == flag))
+
+    def y_relay(n, kh, p):
+        recv(f"r{n}", yrb.at[n])
+        return mine(kh, p) + yrb[n].astype(F32)
+
     def reduce_y(kh):
-        @role(kh, 2)
+        recv(f"rd{kh}", rdb.at[kh])
+        dwm[kh] = dwm[kh] + rdb[kh].astype(F32)
+
+        @role_if(kh, 2, 0)
         def _():
             y_send(0, mine(kh, 0), yn)
             y_send(1, mine(kh, 1), yp)
 
-        @role(kh, 1)
+        @role_if(kh, 1, 0)
         def _():
             y_send(2, mine(kh, 1), yn)
 
-        @role(kh, 3)
+        @role_if(kh, 3, 0)
         def _():
             y_send(3, mine(kh, 0), yp)
 
+        @role_if(kh, 3, 1)
+        def _():
+            y_send(0, mine(kh, 0), yn)
+            y_send(1, mine(kh, 1), yn)
+
     def reduce_y2(kh):
-        @role(kh, 1)
-        def _():
-            recv("r0", yrb.at[0])
-            y_send(4, mine(kh, 0) + yrb[0].astype(F32), yn)
-
-        @role(kh, 3)
-        def _():
-            recv("r1", yrb.at[1])
-            y_send(5, mine(kh, 1) + yrb[1].astype(F32), yp)
+        @role_if(kh, 1, 0)
+        def _():
+            y_send(4, y_relay(0, kh, 0), yn)
+
+        @role_if(kh, 3, 0)
+        def _():
+            y_send(5, y_relay(1, kh, 1), yp)
+
+        @role_if(kh, 2, 1)
+        def _():
+            y_send(2, y_relay(0, kh, 0), yn)
+            y_send(3, y_relay(1, kh, 1), yn)
+
+    def reduce_y3(kh):
+        @role_if(kh, 1, 1)
+        def _():
+            y_send(4, y_relay(2, kh, 0), yn)
+            y_send(5, y_relay(3, kh, 1), yn)
 
     z_refs = [zsb.at[mod(z + k, 8)] for k in range(8)]
 
     def reduce_z(kh):
+        @role_if(kh, 0, 0)
+        def _():
+            recv("r3", yrb.at[3])
+            recv("r2", yrb.at[2])
+            for p in range(2):
+                rows = pl.ds(4 * p, 4)
+                dwm[kh, rows] = mine(kh, p) + yrb[3 - p].astype(F32)
+
         @role(kh, 0)
         def _():
-            for n in range(2, 6):
-                recv(f"r{n}", yrb.at[n])
-            u = kh * 2 + xl
-            lo = mine(kh, 0) + yrb[3].astype(F32) + yrb[4].astype(F32)
-            hi = mine(kh, 1) + yrb[2].astype(F32) + yrb[5].astype(F32)
-            dwm[u, pl.ds(0, 4)] = lo
-            dwm[u, pl.ds(4, 4)] = hi
-            zsb[pl.ds(0, 4)] = lo.astype(BF16)
-            zsb[pl.ds(4, 4)] = hi.astype(BF16)
+            for p in range(2):
+                rows = pl.ds(4 * p, 4)
+                total = y_relay(4 + p, kh, p)
+                dwm[kh, rows] = total
+                zsb[rows] = total.astype(BF16)
             for k in range(1, 8):
                 send(f"rz{k}", z_refs[k], zrb.at[k], zpeer(k))
 
     def reduce_dp():
-        total = dwm[unit(0), z]
+        total = dwm[y, z]
         for k in range(1, 8):
             recv(f"rz{k}", zrb.at[k])
             total = total + zrb[k].astype(F32)
@@ -385,22 +386,21 @@
         sq_ref[...] += jnp.sum((x * x).reshape(TOK // 8, 8, HD), axis=0)
 
     def backward(kh, act_scale):
+        recv(f"xg{kh}", ga.at[kh, 1 - xl])
         sk = [None] * 3
         sv = [None] * 3
         for g in range(GROUP):
             h = kh * GROUP + g
             q = q_ref[:, col(h)]
-            blocks = [wf[8 * h + mod(n + 9 - z, 8)].reshape(32, D_OUT) for n in range(8)]
-            wh = jnp.concatenate(blocks, axis=0)
-            ga = dot_nt(mk[...], wh).astype(BF16)
-            delta = jnp.sum(ga.astype(F32) * at[:, col(h)].astype(F32), axis=1, keepdims=True)
+            gh = ga[kh, g]
+            delta = jnp.sum(gh.astype(F32) * at[h].astype(F32), axis=1, keepdims=True)
             dq = jnp.zeros((TOK, HD), F32)
             for b, (kr, vr) in enumerate(((k2, v2), (k1, v1), (k_ref, v_ref))):
-                dp = dot_nt(ga, vr[:, col(kh)])
+                dp = dot_nt(gh, vr[:, col(kh)])
                 ds = (pw[h, b].astype(F32) * (dp - delta)).astype(BF16)
                 dq = dq + dot_nn(ds, kr[:, col(kh)])
                 dk = dot_tn(ds, q)
-                dv = dot_tn(pb[h, b], ga)
+                dv = dot_tn(pb[h, b], gh)
                 sk[b] = dk if g == 0 else sk[b] + dk
                 sv[b] = dv if g == 0 else sv[b] + dv
             dq = dq * act_scale
@@ -472,43 +472,38 @@
         gather_y(1)
     with jax.named_scope("gather_y0"):
         gather_y0()
-    with jax.named_scope("halo_relay#0"):
-        halo_relay(0)
-    with jax.named_scope("halo_own#1"):
-        unless_last(lambda: halo_own(1))
+    with jax.named_scope("relay_a"):
+        relay_a()
     with jax.named_scope("gather_y1"):
         gather_y1()
     with jax.named_scope("gather_y2#0"):
         gather_y2(0)
+    with jax.named_scope("relay_b"):
+        relay_b()
     with jax.named_scope("gather_y2#1"):
         gather_y2(1)
-    with jax.named_scope("gather_y3"):
-        gather_y3()
     with jax.named_scope("halo_last#0"):
         halo_last(0)
     with jax.named_scope("forward_pair#0"):
         forward_pair(0)
     with jax.named_scope("halo_relay#1"):
-        pl.when(first + last == 0)(lambda: [halo_relay(1), halo_own(2)] and None)
-        pl.when(first == 1)(lambda: halo_own(2))
-    with jax.named_scope("gather_x#0"):
-        gather_x(0)
-    with jax.named_scope("gather_x#1"):
-        gather_x(1)
-    with jax.named_scope("gather_x#3"):
-        gather_x(3)
-    with jax.named_scope("gather_x#2"):
-        gather_x(2)
-    with jax.named_scope("reduce_x#0"):
-        reduce_x(0)
-    with jax.named_scope("gather_done"):
-        gather_done()
-    with jax.named_scope("halo_late#1"):
-        if_last(lambda: [halo_own(1), halo_relay(1), halo_own(2)] and None)
+        halo_relay(1)
+    with jax.named_scope("halo_own#2"):
+        halo_own(2)
+    with jax.named_scope("gather_y3"):
+        gather_y3()
+    with jax.named_scope("project#0"):
+        project(0)
+    with jax.named_scope("project#1"):
+        project(1)
+    with jax.named_scope("weight#0"):
+        weight(0)
+    with jax.named_scope("project#2"):
+        project(2)
+    with jax.named_scope("project#3"):
+        project(3)
     with jax.named_scope("backward#0"):
         backward(0, act_scale)
-    with jax.named_scope("halo_late#0"):
-        pl.when(first == 1)(lambda: halo_relay(1))
     with jax.named_scope("halo_relay#2"):
         halo_relay(2)
     with jax.named_scope("halo_own#3"):
@@ -517,14 +512,12 @@
         halo_last(1)
     with jax.named_scope("forward_pair#1"):
         forward_pair(1)
-    with jax.named_scope("reduce_x_done#0"):
-        reduce_x_done(0)
     with jax.named_scope("reduce_y#0"):
         reduce_y(0)
-    with jax.named_scope("reduce_x#1"):
-        reduce_x(1)
     with jax.named_scope("backward#1"):
         backward(1, act_scale)
+    with jax.named_scope("weight#1"):
+        weight(1)
     with jax.named_scope("combine#0"):
         combine(0)
     with jax.named_scope("halo_relay#3"):
@@ -533,58 +526,60 @@
         halo_last(2)
     with jax.named_scope("forward_pair#2"):
         forward_pair(2)
+    with jax.named_scope("backward#2"):
+        backward(2, act_scale)
     with jax.named_scope("reduce_y2#0"):
         reduce_y2(0)
-    with jax.named_scope("reduce_x_done#1"):
-        reduce_x_done(1)
     with jax.named_scope("reduce_y#1"):
         reduce_y(1)
-    with jax.named_scope("reduce_x#2"):
-        reduce_x(2)
-    with jax.named_scope("backward#2"):
-        backward(2, act_scale)
-    with jax.named_scope("combine#1"):
-        combine(1)
+    with jax.named_scope("weight#2"):
+        weight(2)
     with jax.named_scope("halo_last#3"):
         halo_last(3)
     with jax.named_scope("forward_pair#3"):
         forward_pair(3)
-    with jax.named_scope("reduce_z#0"):
-        reduce_z(0)
+    with jax.named_scope("combine#1"):
+        combine(1)
+    with jax.named_scope("backward#3"):
+        backward(3, act_scale)
     with jax.named_scope("reduce_y2#1"):
         reduce_y2(1)
-    with jax.named_scope("reduce_x_done#2"):
-        reduce_x_done(2)
     with jax.named_scope("reduce_y#2"):
         reduce_y(2)
-    with jax.named_scope("reduce_x#3"):
-        reduce_x(3)
-    with jax.named_scope("backward#3"):
-        backward(3, act_scale)
+    with jax.named_scope("weight#3"):
+        weight(3)
+    with jax.named_scope("reduce_y3#0"):
+        reduce_y3(0)
     with jax.named_scope("combine#2"):
         combine(2)
-    with jax.named_scope("finish#0"):
-        finish(0, act_scale)
-    with jax.named_scope("reduce_z#1"):
-        reduce_z(1)
+    with jax.named_scope("reduce_y#3"):
+        reduce_y(3)
     with jax.named_scope("reduce_y2#2"):
         reduce_y2(2)
-    with jax.named_scope("reduce_x_done#3"):
-        reduce_x_done(3)
-    with jax.named_scope("reduce_y#3"):
-        reduce_y(3)
-    with jax.named_scope("finish#1"):
-        finish(1, act_scale)
-    with jax.named_scope("reduce_z#2"):
-        reduce_z(2)
+    with jax.named_scope("reduce_y3#1"):
+        reduce_y3(1)
     with jax.named_scope("combine#3"):
         combine(3)
     with jax.named_scope("reduce_y2#3"):
         reduce_y2(3)
+    with jax.named_scope("reduce_y3#2"):
+        reduce_y3(2)
+    with jax.named_scope("finish#0"):
+        finish(0, act_scale)
+    with jax.named_scope("reduce_y3#3"):
+        reduce_y3(3)
+    with jax.named_scope("reduce_z#0"):
+        reduce_z(0)
+    with jax.named_scope("reduce_z#1"):
+        reduce_z(1)
+    with jax.named_scope("reduce_z#2"):
+        reduce_z(2)
+    with jax.named_scope("reduce_z#3"):
+        reduce_z(3)
+    with jax.named_scope("finish#1"):
+        finish(1, act_scale)
     with jax.named_scope("finish#2"):
         finish(2, act_scale)
-    with jax.named_scope("reduce_z#3"):
-        reduce_z(3)
     with jax.named_scope("reduce_dp"):
         reduce_dp()
     with jax.named_scope("finish#3"):
@@ -607,19 +602,21 @@
     vm = pl.BlockSpec(memory_space=pltpu.VMEM)
     scratch = [
         ((8, HD), F32),
-        ((64, 2, 16, D_OUT), BF16),
+        ((32, 2, 16, D_OUT), BF16),
         ((TOK, 1024), BF16),
         ((TOK, 1024), BF16),
         ((TOK, 1024), BF16),
         ((TOK, 1024), BF16),
         ((TOK, D_OUT), BF16),
-        ((TOK, 2048), BF16),
+        ((TOK, D_OUT), BF16),
+        ((HEADS, TOK, HD), BF16),
+        ((KV_HEADS, TOK, HD), BF16),
+        ((KV_HEADS, 2, TOK, HD), BF16),
+        ((KV_HEADS, TOK, HD), BF16),
         ((HEADS, 3, TOK, TOK), BF16),
         ((HEADS, 3, TOK, TOK), BF16),
         ((8, 2, 16, D_OUT), F32),
-        ((HEADS, 8, 16, D_OUT), F32),
-        ((HEADS, 8, 16, D_OUT), BF16),
-        ((HEADS, 8, 16, D_OUT), BF16),
+        ((KV_HEADS, 8, 16, D_OUT), F32),
         ((KV_HEADS, 8, 16, D_OUT), BF16),
         ((KV_HEADS, 8, 16, D_OUT), BF16),
         ((6, 4, 16, D_OUT), BF16),

time: 171 us -> 151 us (0.88)
  Pallas kernels: 162 us -> 142 us
    pallas_call x1, Pallas kernels: 162 us -> 142 us  [shards(): pl.pallas_call(body, out_shape=(jax.ShapeDtypeStruct((TOK, 2048), BF16),...]
where the time goes in v3:
time: 151 us
  Pallas kernels  142 us (94%)
  local copies, waits for them, and re-layouts  7.19 us (5%)
    pallas_call x1, Pallas kernels, shards(): pl.pallas_call(body, out_shape=(jax.ShapeDtypeStruct((TOK, 2048), BF16),...  142 us
    unnamed x10, local copies, waits for them, and re-layouts  5.41 us

profile of v3, /device:TPU:1, one launch (start us, length us, event | category | flops | bytes accessed | tf_op | source)
XLA Modules:
  0.0 150.8 jit_solution(14024261313429557237)
XLA Ops:
  1.3 0.6 broadcast_in_dim.12.lt_ref
  1.9 142.3 %band.1 = (bf16[256,2048]{1,0:T(8,128)(2,1)}, bf16[256,1024]{1,0:T(8,128)(2,1)}, bf16[256,1024]{1,0:T(8,128)(2,1)}, f32[2,16,1792]{2,1,0:T(8,128)}, f32[8,128]{1,0:T(8,128)}) custom-call(s32[1]{0:T(128)} %copy.15.len_ref, bf16[256,2048]{1,0:T(8,128)(2,1)} %bitcast.13, bf16[256,1024]{1,0:T(8,128)(2,1)} %bitcast.17, bf16[256,1024]{1,0:T(8,128)(2,1)} %bitcast.18, ...), custom_call_target="tpu_custom_call" | custom-call | tf_op jit(solution)/shard_map/band/pallas_call | solution.py:641
  144.2 1.2 slice.3
  145.4 0.0 copy-start.1
  145.4 2.4 %copy.16 = bf16[1,256,2048]{2,1,0:T(8,128)(2,1)} copy(bf16[1,256,2048]{2,1,0:T(8,128)(2,1)} %bitcast.12) | data formatting | bytes 2097152
  147.7 0.0 copy-done.1
  147.7 0.0 copy-start
  147.7 0.8 copy.17
  148.5 0.4 copy-done
  149.0 0.0 copy-start.2
  149.0 0.8 copy.18
  149.8 0.3 copy-done.2
  150.1 0.7 copy.19
Async XLA Ops:
  145.4 2.4 %copy-start.1 = (bf16[256,1024]{1,0:T(8,128)(2,1)S(1)}, bf16[256,1024]{1,0:T(8,128)(2,1)}, u32[]{:S(2)}) copy-start(bf16[256,1024]{1,0:T(8,128)(2,1)} %get-tuple-element.11) | copy-start | bytes 1572868
  147.7 1.2 copy-start
  149.0 1.1 copy-start.2

commit v4 on v3

--- a/solution.py
+++ b/solution.py
@@ -194,11 +194,25 @@
         recv(f"ov{kh}", v1.at[:, col(kh)])
         send(f"fv{kh}", v1.at[:, col(kh)], v2.at[:, col(kh)], right)
 
+    holds = xl * lax.div(z, 7)
+
     def relay_a():
-        pl.when(z < 7)(lambda: [halo_relay(0), halo_own(1)] and None)
+        pl.when(z == 0)(lambda: [halo_own(1), halo_relay(0), halo_own(2)] and None)
+        pl.when((holds == 0) & (z > 0))(lambda: [halo_relay(0), halo_own(1)] and None)
 
     def relay_b():
-        pl.when(z == 7)(lambda: [halo_relay(0), halo_own(1)] and None)
+        pl.when(holds == 1)(lambda: [halo_relay(0), halo_own(1)] and None)
+
+    def relay_c():
+        pl.when(z == 0)(lambda: halo_own(3))
+        pl.when(z > 0)(lambda: [halo_relay(1), halo_own(2)] and None)
+
+    def relay_d():
+        pl.when(z == 0)(lambda: halo_relay(1))
+
+    def relay_e():
+        halo_relay(2)
+        pl.when(z > 0)(lambda: halo_own(3))
 
     def halo_last(kh):
         recv(f"fk{kh}", k2.at[:, col(kh)])
@@ -348,15 +362,20 @@
                 rows = pl.ds(4 * p, 4)
                 dwm[kh, rows] = mine(kh, p) + yrb[3 - p].astype(F32)
 
-        @role(kh, 0)
-        def _():
-            for p in range(2):
-                rows = pl.ds(4 * p, 4)
+        for p in range(2):
+            rows = pl.ds(4 * p, 4)
+
+            @role(kh, 0)
+            def _():
                 total = y_relay(4 + p, kh, p)
                 dwm[kh, rows] = total
                 zsb[rows] = total.astype(BF16)
+
             for k in range(1, 8):
-                send(f"rz{k}", z_refs[k], zrb.at[k], zpeer(k))
+
+                @pl.when(jnp.logical_and(kh == y, lax.div(mod(z + k, 8), 4) == p))
+                def _():
+                    send(f"rz{k}", z_refs[k], zrb.at[k], zpeer(k))
 
     def reduce_dp():
         total = dwm[y, z]
@@ -476,26 +495,26 @@
         relay_a()
     with jax.named_scope("gather_y1"):
         gather_y1()
+    with jax.named_scope("relay_b"):
+        relay_b()
     with jax.named_scope("gather_y2#0"):
         gather_y2(0)
-    with jax.named_scope("relay_b"):
-        relay_b()
     with jax.named_scope("gather_y2#1"):
         gather_y2(1)
     with jax.named_scope("halo_last#0"):
         halo_last(0)
     with jax.named_scope("forward_pair#0"):
         forward_pair(0)
-    with jax.named_scope("halo_relay#1"):
-        halo_relay(1)
-    with jax.named_scope("halo_own#2"):
-        halo_own(2)
+    with jax.named_scope("relay_c"):
+        relay_c()
     with jax.named_scope("gather_y3"):
         gather_y3()
     with jax.named_scope("project#0"):
         project(0)
     with jax.named_scope("project#1"):
         project(1)
+    with jax.named_scope("relay_d"):
+        relay_d()
     with jax.named_scope("weight#0"):
         weight(0)
     with jax.named_scope("project#2"):
@@ -504,10 +523,8 @@
         project(3)
     with jax.named_scope("backward#0"):
         backward(0, act_scale)
-    with jax.named_scope("halo_relay#2"):
-        halo_relay(2)
-    with jax.named_scope("halo_own#3"):
-        halo_own(3)
+    with jax.named_scope("relay_e"):
+        relay_e()
     with jax.named_scope("halo_last#1"):
         halo_last(1)
     with jax.named_scope("forward_pair#1"):
@@ -532,40 +549,38 @@
         reduce_y2(0)
     with jax.named_scope("reduce_y#1"):
         reduce_y(1)
-    with jax.named_scope("weight#2"):
-        weight(2)
     with jax.named_scope("halo_last#3"):
         halo_last(3)
     with jax.named_scope("forward_pair#3"):
         forward_pair(3)
+    with jax.named_scope("weight#2"):
+        weight(2)
+    with jax.named_scope("backward#3"):
+        backward(3, act_scale)
     with jax.named_scope("combine#1"):
         combine(1)
-    with jax.named_scope("backward#3"):
-        backward(3, act_scale)
+    with jax.named_scope("weight#3"):
+        weight(3)
+    with jax.named_scope("reduce_y#2"):
+        reduce_y(2)
+    with jax.named_scope("reduce_y#3"):
+        reduce_y(3)
     with jax.named_scope("reduce_y2#1"):
         reduce_y2(1)
-    with jax.named_scope("reduce_y#2"):
-        reduce_y(2)
-    with jax.named_scope("weight#3"):
-        weight(3)
+    with jax.named_scope("combine#2"):
+        combine(2)
     with jax.named_scope("reduce_y3#0"):
         reduce_y3(0)
-    with jax.named_scope("combine#2"):
-        combine(2)
-    with jax.named_scope("reduce_y#3"):
-        reduce_y(3)
     with jax.named_scope("reduce_y2#2"):
         reduce_y2(2)
     with jax.named_scope("reduce_y3#1"):
         reduce_y3(1)
-    with jax.named_scope("combine#3"):
-        combine(3)
     with jax.named_scope("reduce_y2#3"):
         reduce_y2(3)
     with jax.named_scope("reduce_y3#2"):
         reduce_y3(2)
-    with jax.named_scope("finish#0"):
-        finish(0, act_scale)
+    with jax.named_scope("combine#3"):
+        combine(3)
     with jax.named_scope("reduce_y3#3"):
         reduce_y3(3)
     with jax.named_scope("reduce_z#0"):
@@ -576,6 +591,8 @@
         reduce_z(2)
     with jax.named_scope("reduce_z#3"):
         reduce_z(3)
+    with jax.named_scope("finish#0"):
+        finish(0, act_scale)
     with jax.named_scope("finish#1"):
         finish(1, act_scale)
     with jax.named_scope("finish#2"):
@@ -596,6 +613,20 @@
                 src_ref=src, dst_ref=src, send_sem=ssem.at[n], recv_sem=rsem.at[n],
                 device_id=cp, device_id_type=MESH,
             ).wait_send()
+
+
+def publish(*refs):
+    given, results, held, sem_in, sem_out = refs[:5], refs[5:10], refs[10:14], refs[14], refs[15]
+    loads = [pltpu.make_async_copy(given[n], held[n], sem_in.at[n]) for n in range(4)]
+    stores = [pltpu.make_async_copy(held[n], results[n], sem_out.at[n]) for n in range(4)]
+    for load in loads:
+        load.start()
+    results[4][0, 0] = given[4][0, 0]
+    for load, store in zip(loads, stores):
+        load.wait()
+        store.start()
+    for store in stores:
+        store.wait()
 
 
 def shards(queries, keys, values, out_grad, out_weight, seq_len):
@@ -652,7 +683,7 @@
         scratch_shapes=[pltpu.VMEM(s, d) for s, d in scratch]
         + [pltpu.SemaphoreType.DMA((CHANNELS,)), pltpu.SemaphoreType.DMA((CHANNELS,))],
         compiler_params=pltpu.CompilerParams(
-            collective_id=0, has_side_effects=True, vmem_limit_bytes=67043328
+            collective_id=0, has_side_effects=True, vmem_limit_bytes=54 * 2**20
         ),
         name="band",
     )(
@@ -664,7 +695,19 @@
         out_weight.reshape(2, 16, D_OUT),
         jnp.full((8, 128), seq_len[0], jnp.int32),
     )
-    return dq[None], dk[None], dv[None], dw.reshape(32, D_OUT), rms[0, 0]
+    shapes = [((TOK, 2048), BF16), ((TOK, 1024), BF16), ((TOK, 1024), BF16), ((32, D_OUT), F32)]
+    anywhere = pl.BlockSpec(memory_space=pl.ANY)
+    scalar = pl.BlockSpec(memory_space=pltpu.SMEM)
+    dq, dk, dv, dw, rms = pl.pallas_call(
+        publish,
+        out_shape=[jax.ShapeDtypeStruct(a, d) for a, d in shapes + [((1, 1), F32)]],
+        in_specs=[anywhere] * 4 + [scalar],
+        out_specs=[anywhere] * 4 + [scalar],
+        scratch_shapes=[pltpu.VMEM(a, d) for a, d in shapes]
+        + [pltpu.SemaphoreType.DMA((4,)), pltpu.SemaphoreType.DMA((4,))],
+        name="publish",
+    )(dq, dk, dv, dw.reshape(32, D_OUT), rms)
+    return dq[None], dk[None], dv[None], dw, rms.reshape(())
 
 
 def solution(mesh):

time: 151 us -> 140 us (0.927)
  local copies, waits for them, and re-layouts: 7.19 us -> 0.59 us
  Pallas kernels: 142 us -> 138 us
    pallas_call x1, Pallas kernels: 142 us -> 134 us  [shards(): pl.pallas_call(body, out_shape=(jax.ShapeDtypeStruct((TOK, 2048), BF16),...]
    unnamed x10 -> x0, local copies, waits for them, and re-layouts: 5.41 us -> none
    pallas_call x0 -> x1, Pallas kernels: none -> 3.91 us  [shards(): pl.pallas_call(publish, out_shape=[jax.ShapeDtypeStruct(a, d) for a, d in...]
where the time goes in v4:
time: 140 us
  Pallas kernels  138 us (99%)
  between operations  1.45 us (1%)
    pallas_call x1, Pallas kernels, shards(): pl.pallas_call(body, out_shape=(jax.ShapeDtypeStruct((TOK, 2048), BF16),...  134 us
    pallas_call x1, Pallas kernels, shards(): pl.pallas_call(publish, out_shape=[jax.ShapeDtypeStruct(a, d) for a, d in...  3.91 us

profile of v4, /device:TPU:1, one launch (start us, length us, event | category | flops | bytes accessed | tf_op | source)
XLA Modules:
  0.0 140.3 jit_solution(9016392305306701837)
XLA Ops:
  1.3 0.6 broadcast_in_dim.12.lt_ref
  1.9 134.3 %band.1 = (bf16[256,2048]{1,0:T(8,128)(2,1)}, bf16[256,1024]{1,0:T(8,128)(2,1)}, bf16[256,1024]{1,0:T(8,128)(2,1)}, f32[2,16,1792]{2,1,0:T(8,128)}, f32[8,128]{1,0:T(8,128)}) custom-call(s32[1]{0:T(128)} %copy.11.len_ref, bf16[256,2048]{1,0:T(8,128)(2,1)} %bitcast.12, bf16[256,1024]{1,0:T(8,128)(2,1)} %bitcast.14, bf16[256,1024]{1,0:T(8,128)(2,1)} %bitcast.15, ...), custom_call_target="tpu_custom_call" | custom-call | tf_op jit(solution)/shard_map/band/pallas_call | solution.py:672
  136.2 3.9 %publish.1 = (bf16[256,2048]{1,0:T(8,128)(2,1)}, bf16[256,1024]{1,0:T(8,128)(2,1)}, bf16[256,1024]{1,0:T(8,128)(2,1)}, f32[32,1792]{1,0:T(8,128)}, f32[1,1]{1,0:T(1,128)}) custom-call(bf16[256,2048]{1,0:T(8,128)(2,1)} %get-tuple-element.15.refs_0_, bf16[256,1024]{1,0:T(8,128)(2,1)} %get-tuple-element.16.refs_1_, ...), custom_call_target="tpu_custom_call" | custom-call | tf_op jit(solution)/shard_map/publish/pallas_call | solution.py:701

commit v5 on v4

--- a/solution.py
+++ b/solution.py
@@ -22,7 +22,8 @@
 SCALE = 0.0625
 CAP = 50.0
 LOG2E = 1.4426950408889634
-CHANNELS = 144
+CHANNELS = 160
+OFFSETS = [(a, b, d) for a in range(4) for b in range(4) for d in range(2) if a + b + d > 0]
 
 F32 = jnp.float32
 BF16 = jnp.bfloat16
@@ -49,7 +50,7 @@
     len_ref, q_ref, k_ref, v_ref, og_ref, w_ref, lt_ref,
     dq_ref, dk_ref, dv_ref, dw_ref, rms_ref,
     sq_ref, wf, k1, k2, v1, v2, mk, mk2, at, at2, ga, gs, pb, pw, tw, dwm, sdb, rdb, ysb, yrb, zsb, zrb,
-    fsb, frb, hsb, hrb, c2s, c2r, cms, cmr, c1, c0, lts, tz, ty, tx, ssem, rsem,
+    fsb, frb, hsb, hrb, c2s, c2r, cms, cmr, c1, c0, lts, tz, tp, ssem, rsem,
 ):
     y, xl, z, xh, c = (lax.axis_index(a) for a in AXES)
     oc = 1 - c
@@ -98,11 +99,16 @@
         ).wait_recv()
 
     barrier = pltpu.get_barrier_semaphore()
-    yo = (mod(y + 2, 4), xl, z, xh, c)
-    xro = (*xr[:4], oc)
-    xpo = (*xp[:4], oc)
-    peers = [zpeer(k) for k in range(1, 8)]
-    peers += [right, left, yn, yp, yo, xr, xp, xro, xpo, x2, x2o, cp]
+    x = xh * 2 + xl
+
+    def plane(dy, dx, dc):
+        there = mod(x + dx, 4)
+        return (mod(y + dy, 4), mod(there, 2), z, lax.div(there, 2), mod(c + dc, 2))
+
+    def plane_slot(dy, dx, dc):
+        return (mod(y + dy + 4, 4) * 4 + mod(x + dx + 4, 4)) * 2 + mod(c + dc, 2)
+
+    peers = [zpeer(k) for k in range(1, 8)] + [plane(*o) for o in OFFSETS] + [right, left]
     for dev in peers:
         pl.semaphore_signal(barrier, inc=1, device_id=dev, device_id_type=MESH)
     pl.semaphore_wait(barrier, len(peers))
@@ -463,16 +469,10 @@
         own = jnp.broadcast_to(own, (8, 128))
         everyone("sz", tz, z, own, [zpeer(k) for k in range(1, 8)])
         total = heard("sz", tz, [mod(z + 8 - k, 8) for k in range(1, 8)])
-        everyone("sy", ty, y, total, [yn, yp, yo])
-        total = heard("sy", ty, [mod(y + 3, 4), mod(y + 1, 4), mod(y + 2, 4)])
-        x = xh * 2 + xl
-        up, down, far = mod(x + 1, 4), mod(x + 3, 4), mod(x + 2, 4)
-        everyone("sx", tx, x * 2 + c, total, [xr, xp, x2, xro, xpo, x2o, cp])
-        slots = [down * 2 + c, up * 2 + c, far * 2 + c]
-        slots += [down * 2 + oc, up * 2 + oc, far * 2 + oc, x * 2 + oc]
-        total = heard("sx", tx, slots)
+        everyone("sp", tp, plane_slot(0, 0, 0), total, [plane(*o) for o in OFFSETS])
+        total = heard("sp", tp, [plane_slot(-dy, -dx, dc) for dy, dx, dc in OFFSETS])
         entries = SLOTS * (HEADS + 2 * KV_HEADS) * HD + HEADS * HD * D_OUT
-        rms_ref[...] = jnp.sqrt(total * (1.0 / entries))
+        rms_ref[0, 0] = jnp.sqrt(total * (1.0 / entries))[0, 0]
 
     sq_ref[...] = jnp.zeros_like(sq_ref)
     with jax.named_scope("gather_z"):
@@ -616,15 +616,19 @@
 
 
 def publish(*refs):
-    given, results, held, sem_in, sem_out = refs[:5], refs[5:10], refs[10:14], refs[14], refs[15]
-    loads = [pltpu.make_async_copy(given[n], held[n], sem_in.at[n]) for n in range(4)]
-    stores = [pltpu.make_async_copy(held[n], results[n], sem_out.at[n]) for n in range(4)]
-    for load in loads:
-        load.start()
+    given, results, sem = refs[:5], refs[5:10], refs[10]
+    rows = TOK // 4
+    pieces = [(n, r) for n in range(3) for r in range(4)]
+    stores = [
+        pltpu.make_async_copy(
+            given[n].at[pl.ds(r * rows, rows)], results[n].at[pl.ds(r * rows, rows)], sem.at[4 * n + r]
+        )
+        for n, r in pieces
+    ]
+    stores.append(pltpu.make_async_copy(given[3], results[3], sem.at[12]))
+    for store in stores:
+        store.start()
     results[4][0, 0] = given[4][0, 0]
-    for load, store in zip(loads, stores):
-        load.wait()
-        store.start()
     for store in stores:
         store.wait()
 
@@ -666,20 +670,19 @@
         ((KV_HEADS, 2, TOK, HD), F32),
         ((3, 8, 128), jnp.int32),
         ((8, 8, 128), F32),
-        ((4, 8, 128), F32),
-        ((8, 8, 128), F32),
+        ((32, 8, 128), F32),
     ]
     dq, dk, dv, dw, rms = pl.pallas_call(
         body,
         out_shape=(
-            jax.ShapeDtypeStruct((TOK, 2048), BF16),
-            jax.ShapeDtypeStruct((TOK, 1024), BF16),
-            jax.ShapeDtypeStruct((TOK, 1024), BF16),
-            jax.ShapeDtypeStruct((2, 16, D_OUT), F32),
-            jax.ShapeDtypeStruct((8, 128), F32),
+            pltpu.VMEM((TOK, 2048), BF16),
+            pltpu.VMEM((TOK, 1024), BF16),
+            pltpu.VMEM((TOK, 1024), BF16),
+            pltpu.VMEM((2, 16, D_OUT), F32),
+            jax.ShapeDtypeStruct((1, 1), F32),
         ),
         in_specs=[pl.BlockSpec(memory_space=pltpu.SMEM)] + [vm] * 6,
-        out_specs=[vm] * 5,
+        out_specs=[vm] * 4 + [pl.BlockSpec(memory_space=pltpu.SMEM)],
         scratch_shapes=[pltpu.VMEM(s, d) for s, d in scratch]
         + [pltpu.SemaphoreType.DMA((CHANNELS,)), pltpu.SemaphoreType.DMA((CHANNELS,))],
         compiler_params=pltpu.CompilerParams(
@@ -695,19 +698,18 @@
         out_weight.reshape(2, 16, D_OUT),
         jnp.full((8, 128), seq_len[0], jnp.int32),
     )
-    shapes = [((TOK, 2048), BF16), ((TOK, 1024), BF16), ((TOK, 1024), BF16), ((32, D_OUT), F32)]
+    shapes = [((TOK, 2048), BF16), ((TOK, 1024), BF16), ((TOK, 1024), BF16), ((2, 16, D_OUT), F32)]
     anywhere = pl.BlockSpec(memory_space=pl.ANY)
     scalar = pl.BlockSpec(memory_space=pltpu.SMEM)
     dq, dk, dv, dw, rms = pl.pallas_call(
         publish,
         out_shape=[jax.ShapeDtypeStruct(a, d) for a, d in shapes + [((1, 1), F32)]],
-        in_specs=[anywhere] * 4 + [scalar],
+        in_specs=[vm] * 4 + [scalar],
         out_specs=[anywhere] * 4 + [scalar],
-        scratch_shapes=[pltpu.VMEM(a, d) for a, d in shapes]
-        + [pltpu.SemaphoreType.DMA((4,)), pltpu.SemaphoreType.DMA((4,))],
+        scratch_shapes=[pltpu.SemaphoreType.DMA((13,))],
         name="publish",
-    )(dq, dk, dv, dw.reshape(32, D_OUT), rms)
-    return dq[None], dk[None], dv[None], dw, rms.reshape(())
+    )(*[pltpu.with_memory_space_constraint(a, pltpu.VMEM) for a in (dq, dk, dv, dw)], rms)
+    return dq[None], dk[None], dv[None], dw.reshape(32, D_OUT), rms.reshape(())
 
 
 def solution(mesh):

time: 140 us -> 137 us (0.979)
  Pallas kernels: 138 us -> 134 us
    pallas_call x1, Pallas kernels: 134 us -> 132 us  [shards(): pl.pallas_call(body, out_shape=(pltpu.VMEM((TOK, 2048), BF16), pltpu.VMEM...]
where the time goes in v5:
time: 137 us
  Pallas kernels  134 us (98%)
  between operations  1.45 us (1%)
    pallas_call x1, Pallas kernels, shards(): pl.pallas_call(body, out_shape=(pltpu.VMEM((TOK, 2048), BF16), pltpu.VMEM...  132 us

profile of v5, /device:TPU:1, one launch (start us, length us, event | category | flops | bytes accessed | tf_op | source)
XLA Modules:
  0.0 136.5 jit_solution(16943387254199488493)
XLA Ops:
  1.3 0.6 broadcast_in_dim.12.lt_ref
  1.9 131.8 %band.1 = (bf16[256,2048]{1,0:T(8,128)(2,1)S(1)}, bf16[256,1024]{1,0:T(8,128)(2,1)S(1)}, bf16[256,1024]{1,0:T(8,128)(2,1)S(1)}, f32[2,16,1792]{2,1,0:T(8,128)S(1)}, f32[1,1]{1,0:T(1,128)}) custom-call(s32[1]{0:T(128)} %copy.11.len_ref, bf16[256,2048]{1,0:T(8,128)(2,1)} %bitcast.12, bf16[256,1024]{1,0:T(8,128)(2,1)} %bitcast.14, bf16[256,1024]{1,0:T(8,128)(2,1)} %bitcast.15, ...), custom_call_target="tpu_custom_call" | custom-call | tf_op jit(solution)/shard_map/band/pallas_call | solution.py:675
  133.7 2.6 %publish.1 = (bf16[256,2048]{1,0:T(8,128)(2,1)}, bf16[256,1024]{1,0:T(8,128)(2,1)}, bf16[256,1024]{1,0:T(8,128)(2,1)}, f32[2,16,1792]{2,1,0:T(8,128)}, f32[1,1]{1,0:T(1,128)}) custom-call(bf16[256,2048]{1,0:T(8,128)(2,1)S(1)} %get-tuple-element.15.refs_0_, bf16[256,1024]{1,0:T(8,128)(2,1)S(1)} %get-tuple-element.16.refs_1_, ...), custom_call_target="tpu_custom_call" | custom-call | tf_op jit(solution)/shard_map/publish/pallas_call | solution.py:704

commit v6 on v5

--- a/solution.py
+++ b/solution.py
@@ -22,7 +22,7 @@
 SCALE = 0.0625
 CAP = 50.0
 LOG2E = 1.4426950408889634
-CHANNELS = 160
+CHANNELS = 78
 OFFSETS = [(a, b, d) for a in range(4) for b in range(4) for d in range(2) if a + b + d > 0]
 
 F32 = jnp.float32
@@ -47,10 +47,10 @@
 
 
 def body(
-    len_ref, q_ref, k_ref, v_ref, og_ref, w_ref, lt_ref,
+    len_ref, q_ref, k_ref, v_ref, og_ref, w_ref,
     dq_ref, dk_ref, dv_ref, dw_ref, rms_ref,
     sq_ref, wf, k1, k2, v1, v2, mk, mk2, at, at2, ga, gs, pb, pw, tw, dwm, sdb, rdb, ysb, yrb, zsb, zrb,
-    fsb, frb, hsb, hrb, c2s, c2r, cms, cmr, c1, c0, lts, tz, tp, ssem, rsem,
+    fsb, frb, hsb, hrb, c2s, c2r, cms, cmr, c1, c0, lt_ref, lts, tz, tp, ssem, rsem,
 ):
     y, xl, z, xh, c = (lax.axis_index(a) for a in AXES)
     oc = 1 - c
@@ -453,12 +453,16 @@
 
     def everyone(name, buf, at_me, value, devs):
         buf[at_me] = value
-        for n, dev in enumerate(devs):
-            send(f"{name}{n}", buf.at[at_me], buf.at[at_me], dev)
-
-    def heard(name, buf, slots):
-        for n, slot in enumerate(slots):
-            recv(f"{name}{n}", buf.at[slot])
+        n = channel(name)
+        for dev in devs:
+            pltpu.make_async_remote_copy(
+                src_ref=buf.at[at_me], dst_ref=buf.at[at_me], send_sem=ssem.at[n],
+                recv_sem=rsem.at[n], device_id=dev, device_id_type=MESH,
+            ).start()
+        sent[name] = (n, buf.at[pl.ds(0, len(devs))])
+
+    def heard(name, buf):
+        recv(name, buf.at[pl.ds(0, buf.shape[0] - 1)])
         total = buf[0]
         for n in range(1, buf.shape[0]):
             total = total + buf[n]
@@ -468,21 +472,22 @@
         own = jnp.sum(jnp.sum(sq_ref[...], axis=0, keepdims=True), axis=1, keepdims=True)
         own = jnp.broadcast_to(own, (8, 128))
         everyone("sz", tz, z, own, [zpeer(k) for k in range(1, 8)])
-        total = heard("sz", tz, [mod(z + 8 - k, 8) for k in range(1, 8)])
+        total = heard("sz", tz)
         everyone("sp", tp, plane_slot(0, 0, 0), total, [plane(*o) for o in OFFSETS])
-        total = heard("sp", tp, [plane_slot(-dy, -dx, dc) for dy, dx, dc in OFFSETS])
+        total = heard("sp", tp)
         entries = SLOTS * (HEADS + 2 * KV_HEADS) * HD + HEADS * HD * D_OUT
         rms_ref[0, 0] = jnp.sqrt(total * (1.0 / entries))[0, 0]
 
+    lt_ref[...] = jnp.full((8, 128), len_ref[0], jnp.int32)
     sq_ref[...] = jnp.zeros_like(sq_ref)
     with jax.named_scope("gather_z"):
         gather_z()
-    with jax.named_scope("lengths_send"):
-        lengths_send()
     with jax.named_scope("halo_own#0"):
         halo_own(0)
     with jax.named_scope("masked"):
         masked()
+    with jax.named_scope("lengths_send"):
+        lengths_send()
     with jax.named_scope("gather_y#0"):
         gather_y(0)
     with jax.named_scope("lengths"):
@@ -567,30 +572,30 @@
         reduce_y(3)
     with jax.named_scope("reduce_y2#1"):
         reduce_y2(1)
-    with jax.named_scope("combine#2"):
-        combine(2)
     with jax.named_scope("reduce_y3#0"):
         reduce_y3(0)
     with jax.named_scope("reduce_y2#2"):
         reduce_y2(2)
+    with jax.named_scope("combine#2"):
+        combine(2)
+    with jax.named_scope("reduce_y2#3"):
+        reduce_y2(3)
     with jax.named_scope("reduce_y3#1"):
         reduce_y3(1)
-    with jax.named_scope("reduce_y2#3"):
-        reduce_y2(3)
     with jax.named_scope("reduce_y3#2"):
         reduce_y3(2)
     with jax.named_scope("combine#3"):
         combine(3)
     with jax.named_scope("reduce_y3#3"):
         reduce_y3(3)
+    with jax.named_scope("reduce_z#3"):
+        reduce_z(3)
     with jax.named_scope("reduce_z#0"):
         reduce_z(0)
     with jax.named_scope("reduce_z#1"):
         reduce_z(1)
     with jax.named_scope("reduce_z#2"):
         reduce_z(2)
-    with jax.named_scope("reduce_z#3"):
-        reduce_z(3)
     with jax.named_scope("finish#0"):
         finish(0, act_scale)
     with jax.named_scope("finish#1"):
@@ -607,6 +612,7 @@
         rms()
     with jax.named_scope("reduce_end"):
         reduce_end()
+    assert len(ids) <= CHANNELS
     with jax.named_scope("drain"):
         for n, src in sent.values():
             pltpu.make_async_remote_copy(
@@ -668,6 +674,7 @@
         ((KV_HEADS, 2, TOK, HD), BF16),
         ((KV_HEADS, 2, TOK, HD), F32),
         ((KV_HEADS, 2, TOK, HD), F32),
+        ((8, 128), jnp.int32),
         ((3, 8, 128), jnp.int32),
         ((8, 8, 128), F32),
         ((32, 8, 128), F32),
@@ -681,7 +688,7 @@
             pltpu.VMEM((2, 16, D_OUT), F32),
             jax.ShapeDtypeStruct((1, 1), F32),
         ),
-        in_specs=[pl.BlockSpec(memory_space=pltpu.SMEM)] + [vm] * 6,
+        in_specs=[pl.BlockSpec(memory_space=pltpu.SMEM)] + [vm] * 5,
         out_specs=[vm] * 4 + [pl.BlockSpec(memory_space=pltpu.SMEM)],
         scratch_shapes=[pltpu.VMEM(s, d) for s, d in scratch]
         + [pltpu.SemaphoreType.DMA((CHANNELS,)), pltpu.SemaphoreType.DMA((CHANNELS,))],
@@ -696,7 +703,6 @@
         values[0],
         out_grad[0],
         out_weight.reshape(2, 16, D_OUT),
-        jnp.full((8, 128), seq_len[0], jnp.int32),
     )
     shapes = [((TOK, 2048), BF16), ((TOK, 1024), BF16), ((TOK, 1024), BF16), ((2, 16, D_OUT), F32)]
     anywhere = pl.BlockSpec(memory_space=pl.ANY)

time: 137 us -> 135 us (0.985)
  no operation moved by 1% of the time
where the time goes in v6:
time: 135 us
  Pallas kernels  133 us (99%)
  between operations  1.45 us (1%)
    pallas_call x1, Pallas kernels, shards(): pl.pallas_call(body, out_shape=(pltpu.VMEM((TOK, 2048), BF16), pltpu.VMEM...  131 us

profile of v6, /device:TPU:1, one launch (start us, length us, event | category | flops | bytes accessed | tf_op | source)
XLA Modules:
  0.0 134.6 jit_solution(18430863825693081717)
XLA Ops:
  1.3 130.5 %band.1 = (bf16[256,2048]{1,0:T(8,128)(2,1)S(1)}, bf16[256,1024]{1,0:T(8,128)(2,1)S(1)}, bf16[256,1024]{1,0:T(8,128)(2,1)S(1)}, f32[2,16,1792]{2,1,0:T(8,128)S(1)}, f32[1,1]{1,0:T(1,128)}) custom-call(s32[1]{0:T(128)S(6)} %copy.11.len_ref, bf16[256,2048]{1,0:T(8,128)(2,1)} %bitcast.10, bf16[256,1024]{1,0:T(8,128)(2,1)} %bitcast.12, ...), custom_call_target="tpu_custom_call" | custom-call | tf_op jit(solution)/shard_map/band/pallas_call | solution.py:682
  131.8 2.6 %publish.1 = (bf16[256,2048]{1,0:T(8,128)(2,1)}, bf16[256,1024]{1,0:T(8,128)(2,1)}, bf16[256,1024]{1,0:T(8,128)(2,1)}, f32[2,16,1792]{2,1,0:T(8,128)}, f32[1,1]{1,0:T(1,128)}) custom-call(bf16[256,2048]{1,0:T(8,128)(2,1)S(1)} %get-tuple-element.15.refs_0_, bf16[256,1024]{1,0:T(8,128)(2,1)S(1)} %get-tuple-element.16.refs_1_, ...), custom_call_target="tpu_custom_call" | custom-call | tf_op jit(solution)/shard_map/publish/pallas_call | solution.py:710
